TPU v7x, 256 devices: a whole 4x4x8 slice. The times are simulated.
256 devices in a mesh: ctx: 32 (over y, z), head: 8 (over x, core).
Axes of the slice: x: 4, y: 4, z: 8, core: 2. Of those that a mesh axis runs over, the one named last changes fastest.
Arguments:
- queries: bfloat16 [65536, 8192], P('ctx', 'head'), may hold values from -9 to 9
- keys: bfloat16 [65536, 1024], P('ctx', 'head'), may hold values from -8 to 8
- values: bfloat16 [65536, 1024], P('ctx', 'head'), may hold values from -6 to 6
- source_block: int32 [512], replicated, may hold values from 0 to 511, as said below
- doc_of_block: int32 [512], replicated, may hold values from 0 to 112, never falling along the last dimension, each value on 1 to 8 neighbouring positions
Outputs:
- attended: bfloat16 [65536, 8192], P(('ctx', 'head'))
Inputs may be any that keep to these rules, and one draw needn't show every extreme that they name: `source_block`: each number once. Generation row block b belongs to generation owner b // 16; pack block p lies on context shard p // 16; a context shard receives at most 1 block from one generation owner. `doc_of_block`: never falling along the pack; a rollout covers 1 to 8 blocks.
All inputs are finite; a program needn't handle non-finite values.
Results may differ from a plain program's by a relative error of at most 0.008.
Values may be sent and summed in bfloat16 or wider, within the bound.
No kernel may reach another device: no remote copies, remote signals or barrier semaphores. Data moves between devices by JAX's collectives and lax.ppermute only.
A program may use at most 64 MiB of HBM per device.

v0:
```python
import jax
import jax.numpy as jnp
from jax import lax
from jax.sharding import PartitionSpec as P

HEAD_SIZE = 128
BLK = 128
DOCMAX = 8


def shifted(block, axis, distance):
    devices = range(lax.axis_size(axis))
    route = [(i - distance, i) for i in devices if i - distance in devices]
    return lax.ppermute(block, axis, route)


def attend(packed_queries, key_extended, value_extended, doc_ext):
    block_total = packed_queries.shape[0] // BLK
    window = DOCMAX * BLK
    key_pos = jnp.arange(window)
    query_pos = (DOCMAX - 1) * BLK + jnp.arange(BLK)
    causal = key_pos[None, :] <= query_pos[:, None]

    def one_block(block_index):
        row_start = block_index * BLK
        query_block = lax.dynamic_slice_in_dim(packed_queries, row_start, BLK, 0)
        key_window = lax.dynamic_slice_in_dim(key_extended, row_start, window, 0)
        value_window = lax.dynamic_slice_in_dim(value_extended, row_start, window, 0)
        window_docs = lax.dynamic_slice_in_dim(doc_ext, block_index, DOCMAX, 0)
        same_doc = window_docs == window_docs[DOCMAX - 1]
        allowed = causal & same_doc[key_pos // BLK][None, :]
        scores = jnp.einsum(
            "qngd,knd->ngqk", query_block, key_window, preferred_element_type=jnp.float32
        ) * HEAD_SIZE ** (-0.5)
        masked = jnp.where(allowed, scores, -1e30)
        row_max = jnp.max(masked, axis=-1, keepdims=True)
        expo_terms = jnp.where(allowed, jnp.exp(masked - row_max), 0.0)
        weights = (expo_terms / jnp.sum(expo_terms, axis=-1, keepdims=True)).astype(jnp.bfloat16)
        mixed_out = jnp.einsum(
            "ngqk,knd->qngd", weights, value_window, preferred_element_type=jnp.float32
        )
        return mixed_out.astype(jnp.bfloat16)

    stacked = lax.map(one_block, jnp.arange(block_total, dtype=jnp.int32))
    return stacked.reshape(packed_queries.shape)


def local(queries, keys, values, source_block, doc_of_block):
    shards = lax.axis_size("ctx")
    own_index = lax.axis_index("ctx")
    row_count = queries.shape[0]
    per_shard = row_count // BLK
    capacity = max(1, per_shard // shards)
    kv_heads = keys.shape[1] // HEAD_SIZE
    query_group_size = queries.shape[1] // keys.shape[1]
    owner_of = (source_block // per_shard).reshape(shards, per_shard)
    local_of = (source_block % per_shard).reshape(shards, per_shard)
    earlier = jnp.arange(per_shard)[None, :] < jnp.arange(per_shard)[:, None]
    same_owner = owner_of[:, :, None] == owner_of[:, None, :]
    rank_of = jnp.sum(same_owner & earlier[None], axis=2)
    matches = (owner_of[:, :, None] == own_index) & (
        rank_of[:, :, None] == jnp.arange(capacity)[None, None, :]
    )
    send_from = jnp.sum(jnp.where(matches, local_of[:, :, None], 0), axis=1).reshape(-1)
    send_live = jnp.any(matches, axis=1).reshape(-1)
    mine_owner = lax.dynamic_index_in_dim(owner_of, own_index, 0, keepdims=False)
    mine_rank = lax.dynamic_index_in_dim(rank_of, own_index, 0, keepdims=False)
    take_from = mine_owner * capacity + mine_rank

    def outgoing(array):
        blocks = array.reshape((per_shard, BLK) + array.shape[1:])
        picked = jnp.take(blocks, send_from, axis=0)
        live = send_live.reshape((-1,) + (1,) * (picked.ndim - 1))
        return jnp.where(live, picked, jnp.zeros((), array.dtype))

    def incoming(array):
        return jnp.take(array, take_from, axis=0).reshape((row_count,) + array.shape[2:])

    query_local = queries.reshape(row_count, kv_heads, query_group_size, HEAD_SIZE)
    key_local = keys.reshape(row_count, kv_heads, HEAD_SIZE)
    value_local = values.reshape(row_count, kv_heads, HEAD_SIZE)
    reach_blocks = DOCMAX - 1
    reachable_rows = reach_blocks * BLK
    global_block = own_index * per_shard - reach_blocks + jnp.arange(reach_blocks + per_shard)
    clipped = jnp.clip(global_block, 0, doc_of_block.shape[0] - 1)
    doc_ext = jnp.where(global_block >= 0, jnp.take(doc_of_block, clipped), -1)
    got_queries, got_keys, got_values = (
        lax.all_to_all(outgoing(query_local), "ctx", split_axis=0, concat_axis=0, tiled=True),
        lax.all_to_all(outgoing(key_local), "ctx", split_axis=0, concat_axis=0, tiled=True),
        lax.all_to_all(outgoing(value_local), "ctx", split_axis=0, concat_axis=0, tiled=True),
    )
    packed_keys = incoming(got_keys)
    packed_values = incoming(got_values)
    earlier_keys, earlier_values = shifted(
        (packed_keys[row_count - reachable_rows :], packed_values[row_count - reachable_rows :]),
        "ctx",
        1,
    )
    key_extended = jnp.concatenate([earlier_keys, packed_keys], axis=0)
    value_extended = jnp.concatenate([earlier_values, packed_values], axis=0)
    key_extended, value_extended = (key_extended, value_extended)
    result = attend(incoming(got_queries), key_extended, value_extended, doc_ext)
    flattened = result.reshape(row_count, queries.shape[1])
    return lax.all_to_all(flattened, "head", split_axis=0, concat_axis=1, tiled=True)


def solution(mesh):
    in_specs = (P("ctx", "head"), P("ctx", "head"), P("ctx", "head"), P(), P())
    out_specs = P(("ctx", "head"), None)
    return jax.shard_map(local, mesh=mesh, in_specs=in_specs, out_specs=out_specs, check_vma=False)
```

profile of v0, /device:TPU:48, one launch (start us, length us, event | category | flops | bytes accessed | tf_op | source)
XLA Modules:
  0.0 612.2 jit_solution(10034387212363410217)
XLA Ops:
  6.1 38.0 %all_to_all.34 = bf16[32,128,1,128]{3,1,2,0:T(8,128)(2,1)S(1)} all-to-all(bf16[32,128,1,128]{3,1,2,0:T(8,128)(2,1)S(1)} %get-tuple-element.215), channel_id=1, replica_groups=mesh['ctx'=32,'head'=8] {'ctx'}, dimensions={0} | all-to-all | bytes 2097152 | tf_op jit(solution)/shard_map/all_to_all | solution.py:89
  44.1 6.6 %all-to-all-start = ((bf16[32,128,1,128]{3,1,2,0:T(8,128)(2,1)}), bf16[32,128,1,128]{3,1,2,0:T(8,128)(2,1)S(1)}, u32[]{:S(2)}, u32[]{:S(2)}) async-start(bf16[32,128,1,128]{3,1,2,0:T(8,128)(2,1)} %get-tuple-element.216), calls=%async_computation | async-start | bytes 2097152 | tf_op jit(solution)/shard_map/all_to_all | solution.py:90
  50.7 5.3 copy.53
  56.0 7.2 %gather_fusion.1 = bf16[32,128,8,128]{3,2,1,0:T(8,128)(2,1)} fusion(bf16[16,128,8,128]{3,2,1,0:T(8,128)(2,1)} %bitcast.148, s32[1024]{0:T(1024)S(1)} %pad_clamp_fusion.1), kind=kCustom, calls=%fused_computation.5 | custom fusion | bytes 16777344 | tf_op jit(solution)/shard_map/jit(_take)/gather | solution.py:72
  63.2 7.6 %fusion.31 = bf16[32,128,1,8,128]{4,3,1,2,0:T(8,128)(2,1)} fusion(bf16[32,128,8,128]{3,2,1,0:T(8,128)(2,1)} %gather_fusion.1, pred[32]{0:T(512)(128)(4,1)S(1)} %compare_and_fusion.1, pred[32]{0:T(512)(128)(4,1)S(1)} %get-tuple-element.201), kind=kLoop, calls=%fused_computation.44 | loop fusion | flops 8388608 | bytes 16777280 | tf_op jit(solution)/shard_map/jit(_where)/select_n | solution.py:74
  70.7 6.6 %all-to-all-done = bf16[32,128,1,128]{3,1,2,0:T(8,128)(2,1)S(1)} async-done(((bf16[32,128,1,128]{3,1,2,0:T(8,128)(2,1)}), bf16[32,128,1,128]{3,1,2,0:T(8,128)(2,1)S(1)}, u32[]{:S(2)}, u32[]{:S(2)}) %all-to-all-start) | async-done | bytes 1048608 | tf_op jit(solution)/shard_map/all_to_all | solution.py:90
  77.3 6.7 %all-to-all-start.2 = ((bf16[32,128,1,8,128]{4,3,1,2,0:T(8,128)(2,1)}), bf16[32,128,1,8,128]{4,3,1,2,0:T(8,128)(2,1)}, u32[]{:S(2)}, u32[]{:S(2)}) async-start(bf16[32,128,1,8,128]{4,3,1,2,0:T(8,128)(2,1)} %fusion.31), calls=%async_computation.2 | async-start | bytes 16777216 | tf_op jit(solution)/shard_map/all_to_all | solution.py:88
  90.0 3.4 collective-permute-start.1
  93.6 184.3 %collective-permute-done = bf16[896,1,128]{2,0,1:T(8,128)(2,1)S(1)} collective-permute-done((bf16[896,1,128]{2,0,1:T(8,128)(2,1)S(1)}, bf16[896,1,128]{2,0,1:T(8,128)(2,1)S(1)}, u32[]{:S(2)}, u32[]{:S(2)}) %collective-permute-start) | collective-permute-done | bytes 229408 | tf_op jit(solution)/shard_map/ppermute | solution.py:14
  281.0 6.4 %gather_fusion.2 = bf16[16,128,8,128]{3,2,1,0:T(8,128)(2,1)} fusion(bf16[32,128,8,128]{3,2,1,0:T(8,128)(2,1)} %bitcast.20, s32[1024]{0:T(1024)S(1)} %pad_clamp_fusion), kind=kCustom, calls=%fused_computation.6 | custom fusion | bytes 8388672 | tf_op jit(solution)/shard_map/jit(_take)/gather | solution.py:77
  287.4 4.2 copy_select_fusion
  291.6 246.3 %while.14 = (s32[]{:T(128)}, bf16[16,128,1,8,128]{4,3,1,0,2:T(8,128)(2,1)}, s32[16]{0:T(128)S(1)}, bf16[2944,1,128]{0,2,1:T(8,128)(2,1)S(1)}, s32[23]{0:T(128)S(...) while((s32[]{:T(128)}, ...), condition=%wide.region_6.9_spmd.clone, body=%wide.region_3.8_spmd.clone.sunk | while | flops 551979008 | bytes 15232410 | solution.py:44
  296.1 4.3 select_reduce_fusion.3
  311.5 4.3 select_reduce_fusion.3
  326.9 4.3 select_reduce_fusion.3
  342.3 4.3 select_reduce_fusion.3
  357.7 4.3 select_reduce_fusion.3
  373.1 4.3 select_reduce_fusion.3
  388.5 4.3 select_reduce_fusion.3
  403.9 4.3 select_reduce_fusion.3
  419.3 4.3 select_reduce_fusion.3
  434.7 4.3 select_reduce_fusion.3
  450.1 4.3 select_reduce_fusion.3
  465.4 4.3 select_reduce_fusion.3
  480.8 4.3 select_reduce_fusion.3
  496.2 4.3 select_reduce_fusion.3
  511.6 4.3 select_reduce_fusion.3
  527.0 4.3 select_reduce_fusion.3
  537.9 7.3 %all_to_all.26 = bf16[8,256,1024]{2,1,0:T(8,128)(2,1)} reshape(bf16[16,128,1,8,128]{4,3,1,0,2:T(8,128)(2,1)} %get-tuple-element.162) | data formatting | bytes 8388608 | tf_op jit(solution)/shard_map/all_to_all | solution.py:104
  545.2 54.1 %all_to_all.35 = bf16[8,256,1024]{2,1,0:T(8,128)(2,1)} all-to-all(bf16[8,256,1024]{2,1,0:T(8,128)(2,1)} %all_to_all.26), channel_id=1, replica_groups=mesh['ctx'=32,'head'=8] {'head'}, dimensions={0} | all-to-all | bytes 8388608 | tf_op jit(solution)/shard_map/all_to_all | solution.py:104
  599.4 6.4 %copy.48 = bf16[256,8,1024]{0,2,1:T(8,128)(2,1)} copy(bf16[256,8,1024]{2,0,1:T(8,128)(2,1)} %bitcast.150) | data formatting | bytes 8388608 | tf_op jit(solution)/shard_map/all_to_all | solution.py:104
  605.8 6.4 %copy.49 = bf16[256,8192]{1,0:T(8,128)(2,1)} copy(bf16[256,8192]{0,1:T(8,128)(2,1)} %bitcast.151) | data formatting | bytes 8388608 | tf_op jit(solution)/shard_map/all_to_all | solution.py:104
  (260 shorter events, 151.8 us)
Async XLA Ops:
  0.0 2.2 copy-start
  44.1 33.2 %all-to-all-start = ((bf16[32,128,1,128]{3,1,2,0:T(8,128)(2,1)}), bf16[32,128,1,128]{3,1,2,0:T(8,128)(2,1)S(1)}, u32[]{:S(2)}, u32[]{:S(2)}) async-start(bf16[32,128,1,128]{3,1,2,0:T(8,128)(2,1)} %get-tuple-element.216), calls=%async_computation | async-start | bytes 2097152 | tf_op jit(solution)/shard_map/all_to_all | solution.py:90
  70.7 13.3 %copy-start.2 = (s32[512]{0:T(512)S(1)}, s32[512]{0:T(512)}, u32[]{:S(2)}) copy-start(s32[512]{0:T(512)} %param.15) | copy-start | bytes 6148
  77.3 203.7 %all-to-all-start.2 = ((bf16[32,128,1,8,128]{4,3,1,2,0:T(8,128)(2,1)}), bf16[32,128,1,8,128]{4,3,1,2,0:T(8,128)(2,1)}, u32[]{:S(2)}, u32[]{:S(2)}) async-start(bf16[32,128,1,8,128]{4,3,1,2,0:T(8,128)(2,1)} %fusion.31), calls=%async_computation.2 | async-start | bytes 16777216 | tf_op jit(solution)/shard_map/all_to_all | solution.py:88
  86.5 191.4 %collective-permute-start = (bf16[896,1,128]{2,0,1:T(8,128)(2,1)S(1)}, bf16[896,1,128]{2,0,1:T(8,128)(2,1)S(1)}, u32[]{:S(2)}, u32[]{:S(2)}) collective-permute-start(bf16[896,1,128]{2,0,1:T(8,128)(2,1)S(1)} %bitcast.158), channel_id=1, source_target_pairs={{0,8},{8,16},{16,24},{24,32},{32,40},{40,48},{48,56},{56,64},{64,7... | collective-permute-start | bytes 688136 | tf_op jit(solution)/shard_map/ppermute | solution.py:14
  90.0 190.9 %collective-permute-start.1 = (bf16[896,1,128]{2,0,1:T(8,128)(2,1)S(1)}, bf16[896,1,128]{2,0,1:T(8,128)(2,1)S(1)}, u32[]{:S(2)}, u32[]{:S(2)}) collective-permute-start(bf16[896,1,128]{2,0,1:T(8,128)(2,1)S(1)} %bitcast.159), channel_id=1, source_target_pairs={{0,8},{8,16},{16,24},{24,32},{32,40},{40,48},{48,56},{56,64},{64,7... | collective-permute-start | bytes 688136 | tf_op jit(solution)/shard_map/ppermute | solution.py:14
  605.8 6.4 %copy-start.1 = (bf16[2048,128]{1,0:T(8,128)(2,1)S(1)}, bf16[2048,128]{1,0:T(8,128)(2,1)}, u32[]{:S(2)}) copy-start(bf16[2048,128]{1,0:T(8,128)(2,1)} %param.13) | copy-start | bytes 1572868
where the time goes:
time: 616 us; the launch traced here: 612 us
  waiting for transfers between devices  194 us (31%)
  other arithmetic  125 us (20%)
  blocking collectives  92.2 us (15%)
  local copies, waits for them, and re-layouts  90.6 us (15%)
  matrix products  49.8 us (8%)
  loops' own time  40.4 us (7%)
  starting transfers between devices  20 us (3%)
    ppermute x2, waiting for transfers between devices, shifted(): return lax.ppermute(block, axis, route)  187 us
    gather x48, other arithmetic, one_block(): allowed = causal & same_doc[key_pos // BLK][None, :]  79.6 us
    all_to_all x1, blocking collectives, local(): lax.all_to_all(flattened, 'head', split_axis=0, concat_axis=1, tiled=True)  54.1 us
    another operation x1, loops' own time, attend(): stacked = lax.map(one_block, jnp.arange(block_total, dtype=jnp.int32))  40.4 us
    all_to_all x1, blocking collectives, local(): lax.all_to_all(outgoing(key_local), 'ctx', split_axis=0, concat_axis=0, t...  38 us
    dot_general x16, matrix products, one_block(): jnp.einsum('qngd,knd->ngqk', query_block, key_window, preferred_element_t...  27.4 us
    dot_general x16, matrix products, one_block(): jnp.einsum('ngqk,knd->qngd', weights, value_window, preferred_element_typ...  22.4 us
    all_to_all x3, local copies, waits for them, and re-layouts, local(): lax.all_to_all(flattened, 'head', split_axis=0, concat_axis=1, tiled=True)  20.1 us
  transfers between devices with their start and end apart: 4, of which 3 were waited for; matrix products, arithmetic and copies ran while one was open for 4% of the time, Pallas kernels for 0%

commit v1 on v0

v1 whole, which is shorter than its diff:
```python
import functools
import math

import jax
import jax.numpy as jnp
from jax import lax
from jax.experimental import pallas as pl
from jax.experimental.pallas import tpu as pltpu
from jax.sharding import PartitionSpec as P


HEAD_SIZE = 128
BLK = 128
DOCMAX = 8
REACH = DOCMAX - 1
ROWS = (64, 48, 16)
TILE = 256
SCALE = HEAD_SIZE**-0.5 * math.log2(math.e)

SMEM = pl.BlockSpec(memory_space=pltpu.SMEM)
VMEM = pl.BlockSpec(memory_space=pltpu.VMEM)
HBM = pl.BlockSpec(memory_space=pl.ANY)


def pack_kv_out(dest, keys, values, out):
    def one(b, carry):
        s = dest[b]
        out[s, :, :HEAD_SIZE] = keys[b]
        out[s, :, HEAD_SIZE:] = values[b]
        return carry

    lax.fori_loop(0, keys.shape[0], one, 0)


def pack_queries(dest, queries, *outs):
    row = 0
    for out in outs:
        rows = out.shape[1]
        out[0] = queries[0, row : row + rows]
        row += rows


def pack_kv_in(owner, got, out):
    def one(b, carry):
        out[b] = got[owner[b]]
        return carry

    lax.fori_loop(0, out.shape[0], one, 0)


def attend(row0, spread, owner, count, seat, got, packed, halo, *refs):
    rows, width = got.shape[1], got.shape[2]
    heads = width // HEAD_SIZE
    blocks = packed.shape[0]
    if spread:
        outs, (out, key_scr, value_scr, sems) = refs[:-4], refs[-4:]
        pair = outs[0].shape[0]
    else:
        out, key_scr, value_scr = refs
    edge = REACH * BLK
    total = blocks * BLK
    key_scr[:edge] = halo[:, :, :HEAD_SIZE].reshape(edge, HEAD_SIZE)
    key_scr[edge:] = packed[:, :, :HEAD_SIZE].reshape(total, HEAD_SIZE)
    value_scr[:edge, :HEAD_SIZE] = halo[:, :, HEAD_SIZE:].reshape(edge, HEAD_SIZE)
    value_scr[edge:, :HEAD_SIZE] = packed[:, :, HEAD_SIZE:].reshape(total, HEAD_SIZE)
    value_scr[:, HEAD_SIZE:] = jnp.ones((edge + total, HEAD_SIZE), value_scr.dtype)
    step = max(d for d in range(1, heads + 1) if heads % d == 0 and d * rows <= TILE)
    row_of = row0 + lax.broadcasted_iota(jnp.int32, (step * rows, BLK), 0) % rows
    allowed = lax.broadcasted_iota(jnp.int32, (step * rows, BLK), 1) <= row_of

    def one(b, carry):
        slot = owner[b]
        if spread:
            at = ((b // pair) ^ seat[0]) * pair + b % pair
        else:
            at = b

        def with_blocks(n):
            start = pl.multiple_of((b + DOCMAX - n) * BLK, BLK)
            k = key_scr[pl.ds(start, n * BLK), :]
            v = value_scr[pl.ds(start, n * BLK), :]
            for first in range(0, heads, step):
                stacked = jnp.concatenate(
                    [
                        got[slot, :, h * HEAD_SIZE : (h + 1) * HEAD_SIZE]
                        for h in range(first, first + step)
                    ],
                    axis=0,
                )
                s = lax.dot_general(
                    stacked, k, (((1,), (1,)), ((), ())), preferred_element_type=jnp.float32
                )
                last = jnp.where(allowed, s[:, (n - 1) * BLK :], -1e30)
                s = last if n == 1 else jnp.concatenate([s[:, : (n - 1) * BLK], last], axis=1)
                m = jnp.max(s, axis=1, keepdims=True)
                p = jnp.exp2((s - m) * SCALE).astype(jnp.bfloat16)
                mixed = jnp.dot(p, v, preferred_element_type=jnp.float32)
                mixed = (mixed[:, :HEAD_SIZE] / mixed[:, HEAD_SIZE:]).astype(jnp.bfloat16)
                for h in range(step):
                    out[at, :, (first + h) * HEAD_SIZE : (first + h + 1) * HEAD_SIZE] = mixed[
                        h * rows : (h + 1) * rows
                    ]

        for n in range(1, DOCMAX + 1):
            pl.when(count[b] == n)(functools.partial(with_blocks, n))
        return carry

    lax.fori_loop(0, blocks, one, 0)
    if spread:
        copies = [
            pltpu.make_async_copy(out.at[pl.ds(k * pair, pair)], outs[k], sems.at[k])
            for k in range(len(outs))
        ]
        for copy in copies:
            copy.start()
        for copy in copies:
            copy.wait()


def place(row0, spread, chained, seat, *refs):
    out, sems = refs[-2], refs[-1]
    parts = refs[: -3 if chained else -2]
    groups = len(parts) if spread else parts[0].shape[0]
    copies = []
    for g in range(groups):
        part = parts[g] if spread else parts[0].at[g]
        h = g ^ seat[0] if spread else g
        pair, rows, width = part.shape
        for i in range(pair):
            copies.append(
                pltpu.make_async_copy(
                    part.at[i],
                    out.at[
                        pl.ds(i * BLK + row0, rows), pl.ds(pl.multiple_of(h * width, width), width)
                    ],
                    sems.at[g, i],
                )
            )
    for copy in copies:
        copy.start()
    for copy in copies:
        copy.wait()


def exchange(queries, keys, values, source_block, doc_of_block):
    shards = lax.axis_size("ctx")
    groups = lax.axis_size("head")
    me = lax.axis_index("ctx")
    seat = lax.axis_index("head").reshape(1)
    row_count, width = queries.shape
    blocks = row_count // BLK
    pair = blocks // groups
    dtype = queries.dtype
    pack_position = jnp.arange(shards * blocks, dtype=jnp.int32)
    held = me * blocks + jnp.arange(blocks, dtype=jnp.int32)
    position = jnp.sum(
        jnp.where(source_block[None, :] == held[:, None], pack_position[None, :], 0), axis=1
    )
    dest = position // blocks

    kv_out = pl.pallas_call(
        pack_kv_out,
        out_shape=jax.ShapeDtypeStruct((shards, BLK, 2 * HEAD_SIZE), dtype),
        in_specs=[SMEM, VMEM, VMEM],
        out_specs=VMEM,
        name="pack_kv_out",
    )(dest, keys.reshape(blocks, BLK, HEAD_SIZE), values.reshape(blocks, BLK, HEAD_SIZE))
    kv_got = lax.all_to_all(kv_out, "ctx", split_axis=0, concat_axis=0, tiled=True)

    q_out = pl.pallas_call(
        pack_queries,
        out_shape=[jax.ShapeDtypeStruct((shards, rows, width), dtype) for rows in ROWS],
        grid_spec=pltpu.PrefetchScalarGridSpec(
            num_scalar_prefetch=1,
            grid=(blocks,),
            in_specs=[pl.BlockSpec((1, BLK, width), lambda b, dest: (b, 0, 0))],
            out_specs=[
                pl.BlockSpec((1, rows, width), lambda b, dest: (dest[b], 0, 0)) for rows in ROWS
            ],
        ),
        name="pack_queries",
    )(dest, queries.reshape(blocks, BLK, width))
    q_got = []
    for q in q_out:
        q_got.append(lax.all_to_all(q, "ctx", split_axis=0, concat_axis=0, tiled=True))

    owner = lax.dynamic_slice_in_dim(source_block, me * blocks, blocks) // blocks
    doc_ext = jnp.concatenate([jnp.full((REACH,), -1, jnp.int32), doc_of_block])
    docs = lax.dynamic_slice_in_dim(doc_ext, me * blocks, blocks + REACH)
    count = sum(
        (docs[REACH - d : REACH - d + blocks] == docs[REACH:]).astype(jnp.int32)
        for d in range(DOCMAX)
    )

    packed = pl.pallas_call(
        pack_kv_in,
        out_shape=jax.ShapeDtypeStruct((blocks, BLK, 2 * HEAD_SIZE), dtype),
        in_specs=[SMEM, VMEM],
        out_specs=VMEM,
        name="pack_kv_in",
    )(owner, kv_got)
    route = [(i, i + 1) for i in range(shards - 1)]
    halo = lax.ppermute(packed[blocks - REACH :], "ctx", route)

    result = None
    row0 = 0
    scratch = [
        pltpu.VMEM(((blocks + REACH) * BLK, HEAD_SIZE), dtype),
        pltpu.VMEM(((blocks + REACH) * BLK, 2 * HEAD_SIZE), dtype),
    ]
    for r, (q, rows) in enumerate(zip(q_got, ROWS)):
        spread = r < len(ROWS) - 1
        if spread:
            shape = [jax.ShapeDtypeStruct((pair, rows, width), dtype)] * groups
            held_out = [pltpu.VMEM((blocks, rows, width), dtype)]
            sems = [pltpu.SemaphoreType.DMA((groups,))]
        else:
            shape = jax.ShapeDtypeStruct((blocks, rows, width), dtype)
            held_out = sems = []
        attended = pl.pallas_call(
            functools.partial(attend, row0, spread),
            out_shape=shape,
            in_specs=[SMEM, SMEM, SMEM, VMEM, VMEM, VMEM],
            out_specs=[HBM] * groups if spread else VMEM,
            scratch_shapes=held_out + scratch + sems,
        )(owner, count, seat, q, packed, halo)
        if spread:
            parts = [attended[0]]
            for k in range(1, groups):
                swap = [(i, i ^ k) for i in range(groups)]
                parts.append(lax.ppermute(attended[k], "head", swap))
        else:
            parts = [
                lax.all_to_all(
                    attended.reshape(groups, pair * rows, width),
                    "head",
                    split_axis=0,
                    concat_axis=0,
                    tiled=True,
                ).reshape(groups, pair, rows, width)
            ]
        before = [] if result is None else [result]
        result = pl.pallas_call(
            functools.partial(place, row0, spread, bool(before)),
            out_shape=jax.ShapeDtypeStruct((pair * BLK, groups * width), dtype),
            in_specs=[SMEM] + [VMEM] * len(parts) + [HBM] * len(before),
            out_specs=HBM,
            scratch_shapes=[pltpu.SemaphoreType.DMA((groups, pair))],
            input_output_aliases={1 + len(parts): 0} if before else {},
        )(seat, *parts, *before)
        row0 += rows
    return result


def solution(mesh):
    in_specs = (P("ctx", "head"), P("ctx", "head"), P("ctx", "head"), P(), P())
    out_specs = P(("ctx", "head"), None)
    return jax.shard_map(exchange, mesh=mesh, in_specs=in_specs, out_specs=out_specs, check_vma=False)
```

time: 616 us -> 388 us (0.63)
  other arithmetic: 125 us -> 3.24 us
  waiting for transfers between devices: 194 us -> 84.5 us
  blocking collectives: 92.2 us -> 180 us
  local copies, waits for them, and re-layouts: 90.6 us -> 4.42 us
  Pallas kernels: 0 us -> 65 us
  matrix products: 49.8 us -> 0 us
  loops' own time: 40.4 us -> 0 us
  starting transfers between devices: 20 us -> 43.7 us
    ppermute x2 -> x15, waiting for transfers between devices: 187 us -> 46.5 us  [the longest x1 23.5 us: exchange(): halo = lax.ppermute(packed[blocks - REACH:], 'ctx', route)]
    all_to_all x2, blocking collectives: 92.2 us -> 180 us  [exchange(): lax.all_to_all(q, 'ctx', split_axis=0, concat_axis=0, tiled=True)]
    gather x53 -> x0, other arithmetic: 79.6 us -> none  [the longest x48 79.6 us: one_block(): allowed = causal & same_doc[key_pos // BLK][None, :]]
    pallas_call x0 -> x9, Pallas kernels: none -> 65 us  [the longest x3 41.2 us: exchange(): pl.pallas_call(functools.partial(attend, row0, spread), out_shape=shape,...]
    dot_general x32 -> x0, matrix products: 49.8 us -> none  [the longest x16 27.4 us: one_block(): jnp.einsum('qngd,knd->ngqk', query_block, key_window, preferred_element_t...]
    another operation x1 -> x0, loops' own time: 40.4 us -> none  [attend(): stacked = lax.map(one_block, jnp.arange(block_total, dtype=jnp.int32))]
    all_to_all x2 -> x3, waiting for transfers between devices: 6.56 us -> 38 us  [the longest x1 38 us: exchange(): lax.all_to_all(kv_out, 'ctx', split_axis=0, concat_axis=0, tiled=True)]
    gather x23 -> x0, local copies, waits for them, and re-layouts: 29 us -> none  [the longest x16 10.9 us: one_block(): allowed = causal & same_doc[key_pos // BLK][None, :]]
  transfers between devices with their start and end apart: 4 -> 18, of which waited for: 3 -> 8; matrix products, arithmetic and copies ran while one was open for 4% -> 1% of each run, Pallas kernels for 0% -> 16%
where the time goes in v1:
time: 388 us; the launch traced here: 381 us
  blocking collectives  180 us (46%)
  waiting for transfers between devices  84.5 us (22%)
  Pallas kernels  65 us (17%)
  starting transfers between devices  43.7 us (11%)
  local copies, waits for them, and re-layouts  4.42 us (1%)
    all_to_all x2, blocking collectives, exchange(): lax.all_to_all(q, 'ctx', split_axis=0, concat_axis=0, tiled=True)  180 us
    pallas_call x3, Pallas kernels, exchange(): pl.pallas_call(functools.partial(attend, row0, spread), out_shape=shape,...  41.2 us
    all_to_all x1, waiting for transfers between devices, exchange(): lax.all_to_all(kv_out, 'ctx', split_axis=0, concat_axis=0, tiled=True)  38 us
    ppermute x1, waiting for transfers between devices, exchange(): halo = lax.ppermute(packed[blocks - REACH:], 'ctx', route)  23.5 us
    ppermute x14, waiting for transfers between devices, exchange(): parts.append(lax.ppermute(attended[k], 'head', swap))  23 us
    ppermute x14, starting transfers between devices, exchange(): parts.append(lax.ppermute(attended[k], 'head', swap))  19 us
    all_to_all x1, starting transfers between devices, exchange(): lax.all_to_all(kv_out, 'ctx', split_axis=0, concat_axis=0, tiled=True)  11.1 us
    pallas_call x1, Pallas kernels, exchange(): pl.pallas_call(pack_queries, out_shape=[jax.ShapeDtypeStruct((shards, row...  10.8 us
  transfers between devices with their start and end apart: 18, of which 8 were waited for; matrix products, arithmetic and copies ran while one was open for 1% of the time, Pallas kernels for 16%

profile of v1, /device:TPU:48, one launch (start us, length us, event | category | flops | bytes accessed | tf_op | source)
XLA Modules:
  0.0 381.4 jit_solution(8354707964752220979)
XLA Ops:
  1.4 2.8 pack_kv_out.1
  4.2 11.1 %all-to-all-start.1 = ((bf16[32,128,256]{2,1,0:T(8,128)(2,1)}), bf16[32,128,256]{2,1,0:T(8,128)(2,1)S(1)}, u32[]{:S(2)}, u32[]{:S(2)}) async-start(bf16[32,128,256]{2,1,0:T(8,128)(2,1)} %pack_kv_out.1), calls=%async_computation.1 | async-start | bytes 4194304 | tf_op jit(solution)/shard_map/all_to_all | solution.py:168
  15.3 10.8 %pack_queries.1 = (bf16[32,64,1024]{2,1,0:T(8,128)(2,1)}, bf16[32,48,1024]{2,1,0:T(8,128)(2,1)}, bf16[32,16,1024]{2,1,0:T(8,128)(2,1)}) custom-call(s32[16]{0:T(128)} %and_select_fusion.dest, bf16[16,128,1024]{2,1,0:T(8,128)(2,1)} %bitcast.6), custom_call_target="tpu_custom_call" | custom-call | tf_op jit(solution)/shard_map/pack_queries/pallas_call | solution.py:170
  26.1 38.0 %all-to-all-done.1.got = bf16[32,128,256]{2,1,0:T(8,128)(2,1)S(1)} async-done(((bf16[32,128,256]{2,1,0:T(8,128)(2,1)}), bf16[32,128,256]{2,1,0:T(8,128)(2,1)S(1)}, u32[]{:S(2)}, u32[]{:S(2)}) %all-to-all-start.1) | async-done | bytes 2097184 | tf_op jit(solution)/shard_map/all_to_all | solution.py:168
  64.1 79.5 %all_to_all.25.got = bf16[32,48,1024]{2,1,0:T(8,128)(2,1)} all-to-all(bf16[32,48,1024]{2,1,0:T(8,128)(2,1)} %get-tuple-element.25), channel_id=1, replica_groups=mesh['ctx'=32,'head'=8] {'ctx'}, dimensions={0} | all-to-all | bytes 6291456 | tf_op jit(solution)/shard_map/all_to_all | solution.py:185
  143.7 100.5 %all_to_all.26.got = bf16[32,64,1024]{2,1,0:T(8,128)(2,1)} all-to-all(bf16[32,64,1024]{2,1,0:T(8,128)(2,1)S(1)} %copy-done.1), channel_id=1, replica_groups=mesh['ctx'=32,'head'=8] {'ctx'}, dimensions={0} | all-to-all | bytes 8388608 | tf_op jit(solution)/shard_map/all_to_all | solution.py:185
  244.2 6.7 %all-to-all-start = ((bf16[32,16,1024]{2,1,0:T(8,128)(2,1)}), bf16[32,16,1024]{2,1,0:T(8,128)(2,1)S(1)}, u32[]{:S(2)}, u32[]{:S(2)}) async-start(bf16[32,16,1024]{2,1,0:T(8,128)(2,1)} %get-tuple-element.24), calls=%async_computation | async-start | bytes 2097152 | tf_op jit(solution)/shard_map/all_to_all | solution.py:185
  251.0 1.2 and_select_fusion.1.owner
  252.2 2.7 pack_kv_in.1.packed
  256.0 3.4 collective-permute-start
  260.0 23.5 %collective-permute-done.halo = bf16[7,128,256]{2,1,0:T(8,128)(2,1)S(1)} collective-permute-done((bf16[7,128,256]{2,1,0:T(8,128)(2,1)S(1)}, bf16[7,128,256]{2,1,0:T(8,128)(2,1)S(1)}, u32[]{:S(2)}, u32[]{:S(2)}) %collective-permute-start) | collective-permute-done | bytes 458784 | tf_op jit(solution)/shard_map/ppermute | solution.py:203
  284.3 15.8 %shard_map.57 = (bf16[2,64,1024]{2,1,0:T(8,128)(2,1)}, bf16[2,64,1024]{2,1,0:T(8,128)(2,1)}, bf16[2,64,1024]{2,1,0:T(8,128)(2,1)}, bf16[2,64,1024]{2,1,0:T(8,128...) custom-call(s32[16]{0:T(128)} %and_select_fusion.1.owner, ...), custom_call_target="tpu_custom_call" | custom-call | tf_op jit(solution)/shard_map/pallas_call | solution.py:220
  300.2 1.8 collective-permute-start.9
  302.0 14.3 %shard_map.56 = (bf16[2,48,1024]{2,1,0:T(8,128)(2,1)}, bf16[2,48,1024]{2,1,0:T(8,128)(2,1)}, bf16[2,48,1024]{2,1,0:T(8,128)(2,1)}, bf16[2,48,1024]{2,1,0:T(8,128...) custom-call(s32[16]{0:T(128)} %and_select_fusion.1.owner, ...), custom_call_target="tpu_custom_call" | custom-call | tf_op jit(solution)/shard_map/pallas_call | solution.py:220
  317.0 1.2 collective-permute-start.10
  318.3 2.7 collective-permute-start.11
  321.0 3.5 collective-permute-done.2.refs_2_
  324.5 1.3 collective-permute-start.12
  326.7 3.2 collective-permute-start.14
  330.9 11.1 %shard_map.55 = bf16[16,16,1024]{2,1,0:T(8,128)(2,1)} custom-call(s32[16]{0:T(128)} %and_select_fusion.1.owner, s32[16]{0:T(128)} %fusion.6.count, s32[1]{0:T(128)} %bitcast.seat, bf16[32,16,1024]{2,1,0:T(8,128)(2,1)} %copy-done.2, bf16[16,128,256]{2,1,0:T(8,128)(2,1)} %pack_kv_in.1.packed, bf16[7,128,256]{2,1,0:T(8,128)(2,1)} %copy-done.3), custom_call_target="tpu_custom_call" | custom-call | tf_op jit(solution)/shard_map/pallas_call | solution.py:220
  341.9 3.5 all-to-all-start.2
  345.5 1.7 collective-permute-start.3
  347.2 2.7 collective-permute-start.4
  350.5 2.1 collective-permute-start.6
  352.5 3.6 collective-permute-done.14.refs_7_
  356.8 2.9 shard_map.58.refs_8_
  359.8 5.0 %collective-permute-done.4.refs_4_ = bf16[2,48,1024]{2,1,0:T(8,128)(2,1)S(1)} collective-permute-done((bf16[2,48,1024]{2,1,0:T(8,128)(2,1)}, bf16[2,48,1024]{2,1,0:T(8,128)(2,1)S(1)}, u32[]{:S(2)}, u32[]{:S(2)}) %collective-permute-start.4) | collective-permute-done | bytes 196640 | tf_op jit(solution)/shard_map/ppermute | solution.py:231
  364.8 3.1 collective-permute-done.5.refs_5_
  367.9 3.3 collective-permute-done.6.refs_6_
  371.2 4.5 %collective-permute-done.7.refs_7_ = bf16[2,48,1024]{2,1,0:T(8,128)(2,1)} collective-permute-done((bf16[2,48,1024]{2,1,0:T(8,128)(2,1)}, bf16[2,48,1024]{2,1,0:T(8,128)(2,1)}, u32[]{:S(2)}, u32[]{:S(2)}) %collective-permute-start.7) | collective-permute-done | bytes 196640 | tf_op jit(solution)/shard_map/ppermute | solution.py:231
  375.7 2.7 shard_map.59.refs_1_
  379.3 2.0 shard_map.60
  (60 shorter events, 8.6 us)
Async XLA Ops:
  4.2 59.9 %all-to-all-start.1 = ((bf16[32,128,256]{2,1,0:T(8,128)(2,1)}), bf16[32,128,256]{2,1,0:T(8,128)(2,1)S(1)}, u32[]{:S(2)}, u32[]{:S(2)}) async-start(bf16[32,128,256]{2,1,0:T(8,128)(2,1)} %pack_kv_out.1), calls=%async_computation.1 | async-start | bytes 4194304 | tf_op jit(solution)/shard_map/all_to_all | solution.py:168
  64.1 180.1 %copy-start = (bf16[32,128,256]{2,1,0:T(8,128)(2,1)}, bf16[32,128,256]{2,1,0:T(8,128)(2,1)S(1)}, u32[]{:S(2)}) copy-start(bf16[32,128,256]{2,1,0:T(8,128)(2,1)S(1)} %all-to-all-done.1.got) | copy-start | bytes 6291460
  64.1 79.5 %copy-start.1 = (bf16[32,64,1024]{2,1,0:T(8,128)(2,1)S(1)}, bf16[32,64,1024]{2,1,0:T(8,128)(2,1)}, u32[]{:S(2)}) copy-start(bf16[32,64,1024]{2,1,0:T(8,128)(2,1)} %get-tuple-element.34) | copy-start | bytes 12582916
  244.2 15.2 %copy-start.17 = (s32[512]{0:T(512)S(1)}, s32[512]{0:T(512)}, u32[]{:S(2)}) copy-start(s32[512]{0:T(512)} %param.9) | copy-start | bytes 6148
  244.2 85.7 %all-to-all-start = ((bf16[32,16,1024]{2,1,0:T(8,128)(2,1)}), bf16[32,16,1024]{2,1,0:T(8,128)(2,1)S(1)}, u32[]{:S(2)}, u32[]{:S(2)}) async-start(bf16[32,16,1024]{2,1,0:T(8,128)(2,1)} %get-tuple-element.24), calls=%async_computation | async-start | bytes 2097152 | tf_op jit(solution)/shard_map/all_to_all | solution.py:185
  256.0 27.6 %collective-permute-start = (bf16[7,128,256]{2,1,0:T(8,128)(2,1)S(1)}, bf16[7,128,256]{2,1,0:T(8,128)(2,1)S(1)}, u32[]{:S(2)}, u32[]{:S(2)}) collective-permute-start(bf16[7,128,256]{2,1,0:T(8,128)(2,1)S(1)} %slice.44), channel_id=1, source_target_pairs={{0,8},{8,16},{16,24},{24,32},{32,40},{40,48},{48,56},{56,64},{64,7... | collective-permute-start | bytes 1376264 | tf_op jit(solution)/shard_map/ppermute | solution.py:203
  300.1 24.4 %copy-start.18 = (bf16[2,64,1024]{2,1,0:T(8,128)(2,1)S(1)}, bf16[2,64,1024]{2,1,0:T(8,128)(2,1)}, u32[]{:S(2)}) copy-start(bf16[2,64,1024]{2,1,0:T(8,128)(2,1)} %get-tuple-element.40) | copy-start | bytes 786436
  300.1 25.7 %collective-permute-start.8 = (bf16[2,64,1024]{2,1,0:T(8,128)(2,1)}, bf16[2,64,1024]{2,1,0:T(8,128)(2,1)S(1)}, u32[]{:S(2)}, u32[]{:S(2)}) collective-permute-start(bf16[2,64,1024]{2,1,0:T(8,128)(2,1)} %get-tuple-element.36), channel_id=1, source_target_pairs={{0,1},{1,0},{2,3},{3,2},{4,5},{5,4},{6,7},{7,6},{8,9},{9,8},{10,11... | collective-permute-start | bytes 786440 | tf_op jit(solution)/shard_map/ppermute | solution.py:231
  300.2 26.5 %collective-permute-start.9 = (bf16[2,64,1024]{2,1,0:T(8,128)(2,1)}, bf16[2,64,1024]{2,1,0:T(8,128)(2,1)S(1)}, u32[]{:S(2)}, u32[]{:S(2)}) collective-permute-start(bf16[2,64,1024]{2,1,0:T(8,128)(2,1)} %get-tuple-element.37), channel_id=1, source_target_pairs={{0,2},{1,3},{2,0},{3,1},{4,6},{5,7},{6,4},{7,5},{8,10},{9,11},{10,... | collective-permute-start | bytes 786440 | tf_op jit(solution)/shard_map/ppermute | solution.py:231
  316.3 2.0 collective-permute-start.1
  316.4 8.1 %collective-permute-start.2 = (bf16[2,48,1024]{2,1,0:T(8,128)(2,1)}, bf16[2,48,1024]{2,1,0:T(8,128)(2,1)S(1)}, u32[]{:S(2)}, u32[]{:S(2)}) collective-permute-start(bf16[2,48,1024]{2,1,0:T(8,128)(2,1)} %get-tuple-element.28), channel_id=1, source_target_pairs={{0,2},{1,3},{2,0},{3,1},{4,6},{5,7},{6,4},{7,5},{8,10},{9,11},{10,... | collective-permute-start | bytes 589832 | tf_op jit(solution)/shard_map/ppermute | solution.py:231
  317.0 28.4 %collective-permute-start.10 = (bf16[2,64,1024]{2,1,0:T(8,128)(2,1)}, bf16[2,64,1024]{2,1,0:T(8,128)(2,1)S(1)}, u32[]{:S(2)}, u32[]{:S(2)}) collective-permute-start(bf16[2,64,1024]{2,1,0:T(8,128)(2,1)} %get-tuple-element.38), channel_id=1, source_target_pairs={{0,3},{1,2},{2,1},{3,0},{4,7},{5,6},{6,5},{7,4},{8,11},{9,10},{10,... | collective-permute-start | bytes 786440 | tf_op jit(solution)/shard_map/ppermute | solution.py:231
  318.3 57.4 %copy-start.12 = (bf16[2,48,1024]{2,1,0:T(8,128)(2,1)}, bf16[2,48,1024]{2,1,0:T(8,128)(2,1)S(1)}, u32[]{:S(2)}) copy-start(bf16[2,48,1024]{2,1,0:T(8,128)(2,1)S(1)} %collective-permute-done.1.refs_1_) | copy-start | bytes 589828
  318.3 28.9 %collective-permute-start.11 = (bf16[2,64,1024]{2,1,0:T(8,128)(2,1)}, bf16[2,64,1024]{2,1,0:T(8,128)(2,1)S(1)}, u32[]{:S(2)}, u32[]{:S(2)}) collective-permute-start(bf16[2,64,1024]{2,1,0:T(8,128)(2,1)} %get-tuple-element.39), channel_id=1, source_target_pairs={{0,4},{1,5},{2,6},{3,7},{4,0},{5,1},{6,2},{7,3},{8,12},{9,13},{10,... | collective-permute-start | bytes 786440 | tf_op jit(solution)/shard_map/ppermute | solution.py:231
  324.5 51.2 %copy-start.13 = (bf16[2,48,1024]{2,1,0:T(8,128)(2,1)}, bf16[2,48,1024]{2,1,0:T(8,128)(2,1)S(1)}, u32[]{:S(2)}) copy-start(bf16[2,48,1024]{2,1,0:T(8,128)(2,1)S(1)} %collective-permute-done.2.refs_2_) | copy-start | bytes 589828
  324.5 25.4 %collective-permute-start.12 = (bf16[2,64,1024]{2,1,0:T(8,128)(2,1)S(1)}, bf16[2,64,1024]{2,1,0:T(8,128)(2,1)S(1)}, u32[]{:S(2)}, u32[]{:S(2)}) collective-permute-start(bf16[2,64,1024]{2,1,0:T(8,128)(2,1)S(1)} %copy-done.18), channel_id=1, source_target_pairs={{0,5},{1,4},{2,7},{3,6},{4,1},{5,0},{6,3},{7,2},{8,13},{9,12},{10,... | collective-permute-start | bytes 786440 | tf_op jit(solution)/shard_map/ppermute | solution.py:231
  325.8 30.3 %copy-start.5 = (bf16[2,64,1024]{2,1,0:T(8,128)(2,1)}, bf16[2,64,1024]{2,1,0:T(8,128)(2,1)S(1)}, u32[]{:S(2)}) copy-start(bf16[2,64,1024]{2,1,0:T(8,128)(2,1)S(1)} %collective-permute-done.8.refs_1_) | copy-start | bytes 786436
  325.8 24.6 %collective-permute-start.13 = (bf16[2,64,1024]{2,1,0:T(8,128)(2,1)}, bf16[2,64,1024]{2,1,0:T(8,128)(2,1)S(1)}, u32[]{:S(2)}, u32[]{:S(2)}) collective-permute-start(bf16[2,64,1024]{2,1,0:T(8,128)(2,1)} %get-tuple-element.41), channel_id=1, source_target_pairs={{0,6},{1,7},{2,4},{3,5},{4,2},{5,3},{6,0},{7,1},{8,14},{9,15},{10,... | collective-permute-start | bytes 786440 | tf_op jit(solution)/shard_map/ppermute | solution.py:231
  326.7 29.4 %copy-start.6 = (bf16[2,64,1024]{2,1,0:T(8,128)(2,1)}, bf16[2,64,1024]{2,1,0:T(8,128)(2,1)S(1)}, u32[]{:S(2)}) copy-start(bf16[2,64,1024]{2,1,0:T(8,128)(2,1)S(1)} %collective-permute-done.9.refs_2_) | copy-start | bytes 786436
  326.7 29.4 %collective-permute-start.14 = (bf16[2,64,1024]{2,1,0:T(8,128)(2,1)}, bf16[2,64,1024]{2,1,0:T(8,128)(2,1)S(1)}, u32[]{:S(2)}, u32[]{:S(2)}) collective-permute-start(bf16[2,64,1024]{2,1,0:T(8,128)(2,1)} %get-tuple-element.42), channel_id=1, source_target_pairs={{0,7},{1,6},{2,5},{3,4},{4,3},{5,2},{6,1},{7,0},{8,15},{9,14},{10,... | collective-permute-start | bytes 786440 | tf_op jit(solution)/shard_map/ppermute | solution.py:231
  341.9 36.5 %all-to-all-start.2 = ((bf16[8,32,1024]{2,1,0:T(8,128)(2,1)}), bf16[8,32,1024]{2,1,0:T(8,128)(2,1)S(1)}, u32[]{:S(2)}, u32[]{:S(2)}) async-start(bf16[8,32,1024]{2,1,0:T(8,128)(2,1)} %bitcast.8), calls=%async_computation.2 | async-start | bytes 1048576 | tf_op jit(solution)/shard_map/all_to_all | solution.py:234
  345.5 10.7 %copy-start.7 = (bf16[2,64,1024]{2,1,0:T(8,128)(2,1)}, bf16[2,64,1024]{2,1,0:T(8,128)(2,1)S(1)}, u32[]{:S(2)}) copy-start(bf16[2,64,1024]{2,1,0:T(8,128)(2,1)S(1)} %collective-permute-done.10.refs_3_) | copy-start | bytes 786436
  345.5 14.3 %collective-permute-start.3 = (bf16[2,48,1024]{2,1,0:T(8,128)(2,1)}, bf16[2,48,1024]{2,1,0:T(8,128)(2,1)S(1)}, u32[]{:S(2)}, u32[]{:S(2)}) collective-permute-start(bf16[2,48,1024]{2,1,0:T(8,128)(2,1)} %get-tuple-element.29), channel_id=1, source_target_pairs={{0,3},{1,2},{2,1},{3,0},{4,7},{5,6},{6,5},{7,4},{8,11},{9,10},{10,... | collective-permute-start | bytes 589832 | tf_op jit(solution)/shard_map/ppermute | solution.py:231
  347.2 8.9 %copy-start.8 = (bf16[2,64,1024]{2,1,0:T(8,128)(2,1)}, bf16[2,64,1024]{2,1,0:T(8,128)(2,1)S(1)}, u32[]{:S(2)}) copy-start(bf16[2,64,1024]{2,1,0:T(8,128)(2,1)S(1)} %collective-permute-done.11.refs_4_) | copy-start | bytes 786436
  347.2 17.6 %collective-permute-start.4 = (bf16[2,48,1024]{2,1,0:T(8,128)(2,1)}, bf16[2,48,1024]{2,1,0:T(8,128)(2,1)S(1)}, u32[]{:S(2)}, u32[]{:S(2)}) collective-permute-start(bf16[2,48,1024]{2,1,0:T(8,128)(2,1)} %get-tuple-element.30), channel_id=1, source_target_pairs={{0,4},{1,5},{2,6},{3,7},{4,0},{5,1},{6,2},{7,3},{8,12},{9,13},{10,... | collective-permute-start | bytes 589832 | tf_op jit(solution)/shard_map/ppermute | solution.py:231
  349.9 6.2 %copy-start.9 = (bf16[2,64,1024]{2,1,0:T(8,128)(2,1)}, bf16[2,64,1024]{2,1,0:T(8,128)(2,1)S(1)}, u32[]{:S(2)}) copy-start(bf16[2,64,1024]{2,1,0:T(8,128)(2,1)S(1)} %collective-permute-done.12.refs_5_) | copy-start | bytes 786436
  349.9 18.0 %collective-permute-start.5 = (bf16[2,48,1024]{2,1,0:T(8,128)(2,1)}, bf16[2,48,1024]{2,1,0:T(8,128)(2,1)S(1)}, u32[]{:S(2)}, u32[]{:S(2)}) collective-permute-start(bf16[2,48,1024]{2,1,0:T(8,128)(2,1)} %get-tuple-element.31), channel_id=1, source_target_pairs={{0,5},{1,4},{2,7},{3,6},{4,1},{5,0},{6,3},{7,2},{8,13},{9,12},{10,... | collective-permute-start | bytes 589832 | tf_op jit(solution)/shard_map/ppermute | solution.py:231
  350.5 20.8 %collective-permute-start.6 = (bf16[2,48,1024]{2,1,0:T(8,128)(2,1)}, bf16[2,48,1024]{2,1,0:T(8,128)(2,1)}, u32[]{:S(2)}, u32[]{:S(2)}) collective-permute-start(bf16[2,48,1024]{2,1,0:T(8,128)(2,1)} %get-tuple-element.32), channel_id=1, source_target_pairs={{0,6},{1,7},{2,4},{3,5},{4,2},{5,3},{6,0},{7,1},{8,14},{9,15},{10,... | collective-permute-start | bytes 589832 | tf_op jit(solution)/shard_map/ppermute | solution.py:231
  356.1 19.6 %collective-permute-start.7 = (bf16[2,48,1024]{2,1,0:T(8,128)(2,1)}, bf16[2,48,1024]{2,1,0:T(8,128)(2,1)}, u32[]{:S(2)}, u32[]{:S(2)}) collective-permute-start(bf16[2,48,1024]{2,1,0:T(8,128)(2,1)} %get-tuple-element.33), channel_id=1, source_target_pairs={{0,7},{1,6},{2,5},{3,4},{4,3},{5,2},{6,1},{7,0},{8,15},{9,14},{10,... | collective-permute-start | bytes 589832 | tf_op jit(solution)/shard_map/ppermute | solution.py:231
  359.8 15.9 %copy-start.14 = (bf16[2,48,1024]{2,1,0:T(8,128)(2,1)}, bf16[2,48,1024]{2,1,0:T(8,128)(2,1)S(1)}, u32[]{:S(2)}) copy-start(bf16[2,48,1024]{2,1,0:T(8,128)(2,1)S(1)} %collective-permute-done.3.refs_3_) | copy-start | bytes 589828
  364.8 10.9 %copy-start.15 = (bf16[2,48,1024]{2,1,0:T(8,128)(2,1)}, bf16[2,48,1024]{2,1,0:T(8,128)(2,1)S(1)}, u32[]{:S(2)}) copy-start(bf16[2,48,1024]{2,1,0:T(8,128)(2,1)S(1)} %collective-permute-done.4.refs_4_) | copy-start | bytes 589828
  367.9 7.8 %copy-start.16 = (bf16[2,48,1024]{2,1,0:T(8,128)(2,1)}, bf16[2,48,1024]{2,1,0:T(8,128)(2,1)S(1)}, u32[]{:S(2)}) copy-start(bf16[2,48,1024]{2,1,0:T(8,128)(2,1)S(1)} %collective-permute-done.5.refs_5_) | copy-start | bytes 589828
  (5 other events, 9.0 us)

commit v2 on v1

v2 whole, which is shorter than its diff:
```python
import functools
import math

import jax
import jax.numpy as jnp
from jax import lax
from jax.experimental import pallas as pl
from jax.experimental.pallas import tpu as pltpu
from jax.sharding import PartitionSpec as P


HEAD_SIZE = 128
BLK = 128
DOCMAX = 8
REACH = DOCMAX - 1
ROWS = (96, 32)
GROUP = (1, 4)
HALVES = 1
COUNTS = (1, 2, 4, 6, 8)
TILE = 384
SCALE = HEAD_SIZE**-0.5 * math.log2(math.e)

SMEM = pl.BlockSpec(memory_space=pltpu.SMEM)
VMEM = pl.BlockSpec(memory_space=pltpu.VMEM)
HBM = pl.BlockSpec(memory_space=pl.ANY)


def pack_kv_out(dest, keys, values, out):
    def one(b, carry):
        s = dest[b]
        out[s, :, :HEAD_SIZE] = keys[b]
        out[s, :, HEAD_SIZE:] = values[b]
        return carry

    lax.fori_loop(0, keys.shape[0], one, 0)


def pack_queries(dest, queries, *outs):
    for r, out in enumerate(outs):
        row = sum(ROWS[:r])
        out[0] = queries[0, row : row + out.shape[1]]


def pack_kv_in(owner, got, out, sems):
    blocks = out.shape[0]
    copies = [
        pltpu.make_async_copy(got.at[owner[b]], out.at[b], sems.at[b]) for b in range(blocks)
    ]
    for copy in copies:
        copy.start()
    for copy in copies:
        copy.wait()


def attend(row0, group, first_seat, spot, owner, count, turn, got, packed, halo, *refs):
    spread = first_seat is not None
    queries, key_scr, value_scr, q_sems = refs[-4:]
    if spread:
        outs, (out, o_sems) = refs[:-6], refs[-6:-4]
        pair = outs[0].shape[0]
    else:
        out = refs[0]
    items, rows, width = out.shape
    blocks = packed.shape[0]
    heads = width // HEAD_SIZE

    def block_at(i):
        if spread:
            return ((first_seat + i // pair) ^ spot[1]) * pair + i % pair
        return turn[i]

    loads = [
        pltpu.make_async_copy(got.at[owner[block_at(i)]], queries.at[i], q_sems.at[i])
        for i in range(items)
    ]
    for load in loads:
        load.start()
    edge = REACH * BLK
    total = blocks * BLK
    key_scr[:edge] = halo[:, :, :HEAD_SIZE].reshape(edge, HEAD_SIZE)
    key_scr[edge:] = packed[:, :, :HEAD_SIZE].reshape(total, HEAD_SIZE)
    value_scr[:edge, :HEAD_SIZE] = halo[:, :, HEAD_SIZE:].reshape(edge, HEAD_SIZE)
    value_scr[edge:, :HEAD_SIZE] = packed[:, :, HEAD_SIZE:].reshape(total, HEAD_SIZE)
    value_scr[:, HEAD_SIZE:] = jnp.ones((edge + total, HEAD_SIZE), value_scr.dtype)
    step = max(d for d in range(1, heads + 1) if heads % d == 0 and d * rows <= TILE)
    row_of = row0 + lax.broadcasted_iota(jnp.int32, (step * rows, BLK), 0) % rows
    allowed = lax.broadcasted_iota(jnp.int32, (step * rows, BLK), 1) <= row_of
    for load in loads:
        load.wait()

    def some(i, carry):
        held = [(i * group + g, block_at(i * group + g)) for g in range(group)]
        most = count[held[0][1]]
        for _, b in held[1:]:
            most = jnp.maximum(most, count[b])

        def with_blocks(n):
            work = []
            for item, b in held:
                start = pl.multiple_of((b + DOCMAX - n) * BLK, BLK)
                k = key_scr[pl.ds(start, n * BLK), :]
                for first in range(0, heads, step):
                    stacked = jnp.concatenate(
                        [
                            queries[item, :, h * HEAD_SIZE : (h + 1) * HEAD_SIZE]
                            for h in range(first, first + step)
                        ],
                        axis=0,
                    )
                    s = lax.dot_general(
                        stacked, k, (((1,), (1,)), ((), ())), preferred_element_type=jnp.float32
                    )
                    work.append((item if spread else b, b, start, first, s))
            weighted = []
            for _, b, start, first, s in work:
                parts = [
                    s[:, j * BLK : (j + 1) * BLK] + jnp.where(n - j <= count[b], 0.0, -1e30)
                    for j in range(n - 1)
                ]
                parts.append(jnp.where(allowed, s[:, (n - 1) * BLK :], -1e30))
                m = functools.reduce(jnp.maximum, parts)
                m = jnp.max(m, axis=1, keepdims=True)
                p = [jnp.exp2((part - m) * SCALE).astype(jnp.bfloat16) for part in parts]
                p = p[0] if n == 1 else jnp.concatenate(p, axis=1)
                weighted.append(p)
            for (at, _, start, first, _), p in zip(work, weighted):
                v = value_scr[pl.ds(start, n * BLK), :]
                mixed = jnp.dot(p, v, preferred_element_type=jnp.float32)
                mixed = (mixed[:, :HEAD_SIZE] / mixed[:, HEAD_SIZE:]).astype(jnp.bfloat16)
                for h in range(step):
                    out[at, :, (first + h) * HEAD_SIZE : (first + h + 1) * HEAD_SIZE] = mixed[
                        h * rows : (h + 1) * rows
                    ]

        low = 0
        for n in COUNTS:
            pl.when((most > low) & (most <= n))(functools.partial(with_blocks, n))
            low = n
        return carry

    lax.fori_loop(0, items // group, some, 0)
    if spread:
        copies = [
            pltpu.make_async_copy(out.at[pl.ds(k * pair, pair)], outs[k], o_sems.at[k])
            for k in range(len(outs))
        ]
        for copy in copies:
            copy.start()
        for copy in copies:
            copy.wait()


def place(row0, spread, chained, spot, *refs):
    out, sems = refs[-2], refs[-1]
    parts = refs[: -3 if chained else -2]
    groups = len(parts) if spread else parts[0].shape[0]
    copies = []
    for g in range(groups):
        part = parts[g] if spread else parts[0].at[g]
        h = g ^ spot[1] if spread else g
        pair, rows, width = part.shape
        for i in range(pair):
            copies.append(
                pltpu.make_async_copy(
                    part.at[i],
                    out.at[
                        pl.ds(i * BLK + row0, rows), pl.ds(pl.multiple_of(h * width, width), width)
                    ],
                    sems.at[g, i],
                )
            )
    for copy in copies:
        copy.start()
    for copy in copies:
        copy.wait()


def exchange(queries, keys, values, source_block, doc_of_block):
    shards = lax.axis_size("ctx")
    groups = lax.axis_size("head")
    me = lax.axis_index("ctx")
    spot = jnp.stack([me, lax.axis_index("head")])
    row_count, width = queries.shape
    blocks = row_count // BLK
    pair = blocks // groups
    dtype = queries.dtype
    pack_position = jnp.arange(shards * blocks, dtype=jnp.int32)
    held = me * blocks + jnp.arange(blocks, dtype=jnp.int32)
    position = jnp.sum(
        jnp.where(source_block[None, :] == held[:, None], pack_position[None, :], 0), axis=1
    )
    dest = position // blocks

    kv_out = pl.pallas_call(
        pack_kv_out,
        out_shape=jax.ShapeDtypeStruct((shards, BLK, 2 * HEAD_SIZE), dtype),
        in_specs=[SMEM, VMEM, VMEM],
        out_specs=VMEM,
        name="pack_kv_out",
    )(dest, keys.reshape(blocks, BLK, HEAD_SIZE), values.reshape(blocks, BLK, HEAD_SIZE))
    kv_got = lax.all_to_all(kv_out, "ctx", split_axis=0, concat_axis=0, tiled=True)

    query_blocks = queries.reshape(blocks, BLK, width)
    q_out = pl.pallas_call(
        pack_queries,
        out_shape=[jax.ShapeDtypeStruct((shards, rows, width), dtype) for rows in ROWS],
        grid_spec=pltpu.PrefetchScalarGridSpec(
            num_scalar_prefetch=1,
            grid=(blocks,),
            in_specs=[pl.BlockSpec((1, BLK, width), lambda b, dest: (b, 0, 0))],
            out_specs=[
                pl.BlockSpec((1, rows, width), lambda b, dest: (dest[b], 0, 0)) for rows in ROWS
            ],
        ),
        name="pack_queries",
    )(dest, query_blocks)
    q_got = []
    for q in q_out:
        q_got.append(lax.all_to_all(q, "ctx", split_axis=0, concat_axis=0, tiled=True))

    owner = lax.dynamic_slice_in_dim(source_block, me * blocks, blocks) // blocks
    doc_ext = jnp.concatenate([jnp.full((REACH,), -1, jnp.int32), doc_of_block])
    docs = lax.dynamic_slice_in_dim(doc_ext, me * blocks, blocks + REACH)
    count = sum(
        (docs[REACH - d : REACH - d + blocks] == docs[REACH:]).astype(jnp.int32)
        for d in range(DOCMAX)
    )
    at = jnp.arange(blocks, dtype=jnp.int32)
    key = count * blocks + at
    rank = jnp.sum((key[None, :] < key[:, None]).astype(jnp.int32), axis=1)
    turn = jnp.sum(jnp.where(rank[None, :] == at[:, None], at[None, :], 0), axis=1)

    packed = pl.pallas_call(
        pack_kv_in,
        out_shape=jax.ShapeDtypeStruct((blocks, BLK, 2 * HEAD_SIZE), dtype),
        in_specs=[SMEM, HBM],
        out_specs=VMEM,
        scratch_shapes=[pltpu.SemaphoreType.DMA((blocks,))],
        name="pack_kv_in",
    )(owner, kv_got)
    route = [(i, i + 1) for i in range(shards - 1)]
    halo = lax.ppermute(packed[blocks - REACH :], "ctx", route)

    result = None
    row0 = 0
    for r, (got, rows) in enumerate(zip(q_got, ROWS)):
        spread = r < len(ROWS) - 1
        step = groups // HALVES if spread else groups
        parts = [None] * groups
        for first in reversed(range(0, groups, step)):
            items = step * pair
            scratch = [
                pltpu.VMEM((items, rows, width), dtype),
                pltpu.VMEM(((blocks + REACH) * BLK, HEAD_SIZE), dtype),
                pltpu.VMEM(((blocks + REACH) * BLK, 2 * HEAD_SIZE), dtype),
                pltpu.SemaphoreType.DMA((items,)),
            ]
            if spread:
                shape = [jax.ShapeDtypeStruct((pair, rows, width), dtype)] * step
                scratch = [
                    pltpu.VMEM((items, rows, width), dtype),
                    pltpu.SemaphoreType.DMA((step,)),
                ] + scratch
            else:
                shape = jax.ShapeDtypeStruct((blocks, rows, width), dtype)
            attended = pl.pallas_call(
                functools.partial(attend, row0, GROUP[r], first if spread else None),
                out_shape=shape,
                in_specs=[SMEM] * 4 + [HBM, VMEM, VMEM],
                out_specs=[HBM] * step if spread else VMEM,
                scratch_shapes=scratch,
            )(spot, owner, count, turn, got, packed, halo)
            if spread:
                for k in range(first, first + step):
                    swap = [(i, i ^ k) for i in range(groups)]
                    part = attended[k - first]
                    parts[k] = lax.ppermute(part, "head", swap) if k else part
            else:
                parts = [
                    lax.all_to_all(
                        attended.reshape(groups, pair * rows, width),
                        "head",
                        split_axis=0,
                        concat_axis=0,
                        tiled=True,
                    ).reshape(groups, pair, rows, width)
                ]
        before = [] if result is None else [result]
        result = pl.pallas_call(
            functools.partial(place, row0, spread, bool(before)),
            out_shape=jax.ShapeDtypeStruct((pair * BLK, groups * width), dtype),
            in_specs=[SMEM] + [VMEM] * len(parts) + [HBM] * len(before),
            out_specs=HBM,
            scratch_shapes=[pltpu.SemaphoreType.DMA((groups, pair))],
            input_output_aliases={1 + len(parts): 0} if before else {},
        )(spot, *parts, *before)
        row0 += rows
    return result


def solution(mesh):
    in_specs = (P("ctx", "head"), P("ctx", "head"), P("ctx", "head"), P(), P())
    out_specs = P(("ctx", "head"), None)
    return jax.shard_map(exchange, mesh=mesh, in_specs=in_specs, out_specs=out_specs, check_vma=False)
```

time: 388 us -> 363 us (0.936)
  waiting for transfers between devices: 84.5 us -> 209 us
  blocking collectives: 180 us -> 56.8 us
  Pallas kernels: 65 us -> 48.1 us
  starting transfers between devices: 43.7 us -> 35.7 us
    all_to_all x2 -> x1, blocking collectives: 180 us -> 56.8 us  [exchange(): lax.all_to_all(q, 'ctx', split_axis=0, concat_axis=0, tiled=True)]
    ppermute x1, waiting for transfers between devices: 23.5 us -> 138 us  [exchange(): halo = lax.ppermute(packed[blocks - REACH:], 'ctx', route)]
    pallas_call x3 -> x2, Pallas kernels: 41.2 us -> 25.5 us  [exchange(): pl.pallas_call(functools.partial(attend, row0, GROUP[r], first if spread...]
    ppermute x14 -> x7, waiting for transfers between devices: 23 us -> 33.2 us  [exchange(): parts[k] = lax.ppermute(part, 'head', swap) if k else part]
    ppermute x14 -> x7, starting transfers between devices: 19 us -> 10 us  [exchange(): parts[k] = lax.ppermute(part, 'head', swap) if k else part]
  transfers between devices with their start and end apart: 18 -> 11, of which waited for: 8 -> 7; matrix products, arithmetic and copies ran while one was open for 1% -> 1% of each run, Pallas kernels for 16% -> 12%
where the time goes in v2:
time: 363 us; the launch traced here: 358 us
  waiting for transfers between devices  209 us (58%)
  blocking collectives  56.8 us (16%)
  Pallas kernels  48.1 us (13%)
  starting transfers between devices  35.7 us (10%)
  other arithmetic  4.68 us (1%)
    ppermute x1, waiting for transfers between devices, exchange(): halo = lax.ppermute(packed[blocks - REACH:], 'ctx', route)  138 us
    all_to_all x1, blocking collectives, exchange(): lax.all_to_all(q, 'ctx', split_axis=0, concat_axis=0, tiled=True)  56.8 us
    all_to_all x1, waiting for transfers between devices, exchange(): lax.all_to_all(kv_out, 'ctx', split_axis=0, concat_axis=0, tiled=True)  38 us
    ppermute x7, waiting for transfers between devices, exchange(): parts[k] = lax.ppermute(part, 'head', swap) if k else part  33.2 us
    pallas_call x2, Pallas kernels, exchange(): pl.pallas_call(functools.partial(attend, row0, GROUP[r], first if spread...  25.5 us
    all_to_all x1, starting transfers between devices, exchange(): lax.all_to_all(kv_out, 'ctx', split_axis=0, concat_axis=0, tiled=True)  11.1 us
    pallas_call x1, Pallas kernels, exchange(): pl.pallas_call(pack_queries, out_shape=[jax.ShapeDtypeStruct((shards, row...  10.8 us
    ppermute x7, starting transfers between devices, exchange(): parts[k] = lax.ppermute(part, 'head', swap) if k else part  10 us
  transfers between devices with their start and end apart: 11, of which 7 were waited for; matrix products, arithmetic and copies ran while one was open for 1% of the time, Pallas kernels for 12%

profile of v2, /device:TPU:48, one launch (start us, length us, event | category | flops | bytes accessed | tf_op | source)
XLA Modules:
  0.0 357.5 jit_solution(11165393148691170185)
XLA Ops:
  0.0 0.9 select_reduce_fusion
  1.4 2.8 pack_kv_out.1
  4.2 11.1 %all-to-all-start.1 = ((bf16[32,128,256]{2,1,0:T(8,128)(2,1)}), bf16[32,128,256]{2,1,0:T(8,128)(2,1)S(1)}, u32[]{:S(2)}, u32[]{:S(2)}) async-start(bf16[32,128,256]{2,1,0:T(8,128)(2,1)} %pack_kv_out.1), calls=%async_computation.1 | async-start | bytes 4194304 | tf_op jit(solution)/shard_map/all_to_all | solution.py:201
  15.3 10.8 %pack_queries.1 = (bf16[32,96,1024]{2,1,0:T(8,128)(2,1)}, bf16[32,32,1024]{2,1,0:T(8,128)(2,1)}) custom-call(s32[16]{0:T(128)} %and_select_fusion.dest, bf16[16,128,1024]{2,1,0:T(8,128)(2,1)} %bitcast.8), custom_call_target="tpu_custom_call" | custom-call | tf_op jit(solution)/shard_map/pack_queries/pallas_call | solution.py:204
  26.1 38.0 %all-to-all-done.1.got = bf16[32,128,256]{2,1,0:T(8,128)(2,1)S(1)} async-done(((bf16[32,128,256]{2,1,0:T(8,128)(2,1)}), bf16[32,128,256]{2,1,0:T(8,128)(2,1)S(1)}, u32[]{:S(2)}, u32[]{:S(2)}) %all-to-all-start.1) | async-done | bytes 2097184 | tf_op jit(solution)/shard_map/all_to_all | solution.py:201
  64.1 56.8 %all_to_all.20.got = bf16[32,32,1024]{2,1,0:T(8,128)(2,1)} all-to-all(bf16[32,32,1024]{2,1,0:T(8,128)(2,1)} %get-tuple-element.15), channel_id=1, replica_groups=mesh['ctx'=32,'head'=8] {'ctx'}, dimensions={0} | all-to-all | bytes 4194304 | tf_op jit(solution)/shard_map/all_to_all | solution.py:219
  120.9 6.8 %all-to-all-start.3 = ((bf16[32,96,1024]{2,1,0:T(8,128)(2,1)}), bf16[32,96,1024]{2,1,0:T(8,128)(2,1)}, u32[]{:S(2)}, u32[]{:S(2)}) async-start(bf16[32,96,1024]{2,1,0:T(8,128)(2,1)} %get-tuple-element.16), calls=%async_computation.3 | async-start | bytes 12582912 | tf_op jit(solution)/shard_map/all_to_all | solution.py:219
  127.8 1.3 and_select_fusion.1.owner
  129.0 0.6 pad_add_fusion.spot
  129.6 3.0 pack_kv_in.1.packed
  132.6 1.1 slice.44
  133.7 3.4 collective-permute-start
  137.1 0.7 iota_add_fusion.1
  138.0 0.6 select_reduce_fusion.1.turn
  138.6 137.9 %collective-permute-done.halo = bf16[7,128,256]{2,1,0:T(8,128)(2,1)S(1)} collective-permute-done((bf16[7,128,256]{2,1,0:T(8,128)(2,1)S(1)}, bf16[7,128,256]{2,1,0:T(8,128)(2,1)S(1)}, u32[]{:S(2)}, u32[]{:S(2)}) %collective-permute-start) | collective-permute-done | bytes 458784 | tf_op jit(solution)/shard_map/ppermute | solution.py:242
  276.5 0.8 copy-done.2
  277.3 7.8 %shard_map.55 = bf16[16,32,1024]{2,1,0:T(8,128)(2,1)} custom-call(s32[2]{0:T(128)} %pad_add_fusion.spot, s32[16]{0:T(128)} %and_select_fusion.1.owner, s32[16]{0:T(128)} %get-tuple-element.26.count, s32[16]{0:T(128)} %select_reduce_fusion.1.turn, bf16[32,32,1024]{2,1,0:T(8,128)(2,1)} %all_to_all.20.got, bf16[16,128,256]{2,1,0:T(8,128)(2,1)} %pack_kv_in.1.packed, ...), custom_call_target="tpu_custom_call" | custom-call | tf_op jit(solution)/shard_map/pallas_call | solution.py:266
  285.1 4.3 %all-to-all-start.2 = ((bf16[8,64,1024]{2,1,0:T(8,128)(2,1)}), bf16[8,64,1024]{2,1,0:T(8,128)(2,1)S(1)}, u32[]{:S(2)}, u32[]{:S(2)}) async-start(bf16[8,64,1024]{2,1,0:T(8,128)(2,1)} %bitcast.9), calls=%async_computation.2 | async-start | bytes 2097152 | tf_op jit(solution)/shard_map/all_to_all | solution.py:280
  289.4 17.7 %shard_map.56 = (bf16[2,96,1024]{2,1,0:T(8,128)(2,1)}, bf16[2,96,1024]{2,1,0:T(8,128)(2,1)}, bf16[2,96,1024]{2,1,0:T(8,128)(2,1)}, bf16[2,96,1024]{2,1,0:T(8,128...) custom-call(s32[2]{0:T(128)} %pad_add_fusion.spot, ...), custom_call_target="tpu_custom_call" | custom-call | tf_op jit(solution)/shard_map/pallas_call | solution.py:266
  307.1 0.8 collective-permute-start.1
  308.0 1.6 collective-permute-start.2
  309.6 3.2 collective-permute-start.4
  313.0 2.8 collective-permute-start.6
  315.8 4.4 %collective-permute-done.2.refs_2_ = bf16[2,96,1024]{2,1,0:T(8,128)(2,1)S(1)} collective-permute-done((bf16[2,96,1024]{2,1,0:T(8,128)(2,1)}, bf16[2,96,1024]{2,1,0:T(8,128)(2,1)S(1)}, u32[]{:S(2)}, u32[]{:S(2)}) %collective-permute-start.2) | collective-permute-done | bytes 393248 | tf_op jit(solution)/shard_map/ppermute | solution.py:277
  320.2 1.4 collective-permute-start.7
  321.6 6.3 %collective-permute-done.3.refs_3_ = bf16[2,96,1024]{2,1,0:T(8,128)(2,1)S(1)} collective-permute-done((bf16[2,96,1024]{2,1,0:T(8,128)(2,1)}, bf16[2,96,1024]{2,1,0:T(8,128)(2,1)S(1)}, u32[]{:S(2)}, u32[]{:S(2)}) %collective-permute-start.3) | collective-permute-done | bytes 393248 | tf_op jit(solution)/shard_map/ppermute | solution.py:277
  327.8 11.5 %collective-permute-done.4.refs_4_ = bf16[2,96,1024]{2,1,0:T(8,128)(2,1)S(1)} collective-permute-done((bf16[2,96,1024]{2,1,0:T(8,128)(2,1)}, bf16[2,96,1024]{2,1,0:T(8,128)(2,1)S(1)}, u32[]{:S(2)}, u32[]{:S(2)}) %collective-permute-start.4) | collective-permute-done | bytes 393248 | tf_op jit(solution)/shard_map/ppermute | solution.py:277
  339.4 7.3 %collective-permute-done.5.refs_5_ = bf16[2,96,1024]{2,1,0:T(8,128)(2,1)S(1)} collective-permute-done((bf16[2,96,1024]{2,1,0:T(8,128)(2,1)}, bf16[2,96,1024]{2,1,0:T(8,128)(2,1)S(1)}, u32[]{:S(2)}, u32[]{:S(2)}) %collective-permute-start.5) | collective-permute-done | bytes 393248 | tf_op jit(solution)/shard_map/ppermute | solution.py:277
  346.7 3.7 %collective-permute-done.7.refs_7_ = bf16[2,96,1024]{2,1,0:T(8,128)(2,1)} collective-permute-done((bf16[2,96,1024]{2,1,0:T(8,128)(2,1)}, bf16[2,96,1024]{2,1,0:T(8,128)(2,1)}, u32[]{:S(2)}, u32[]{:S(2)}) %collective-permute-start.7) | collective-permute-done | bytes 393248 | tf_op jit(solution)/shard_map/ppermute | solution.py:277
  350.4 3.6 %shard_map.57.refs_1_ = bf16[256,8192]{1,0:T(8,128)(2,1)} custom-call(s32[2]{0:T(128)} %pad_add_fusion.spot, bf16[2,96,1024]{2,1,0:T(8,128)(2,1)} %get-tuple-element.17.refs_0_, bf16[2,96,1024]{2,1,0:T(8,128)(2,1)} %copy-done.3, bf16[2,96,1024]{2,1,0:T(8,128)(2,1)} %copy-done.4, bf16[2,96,1024]{2,1,0:T(8,128)(2,1)} %copy-done.5, ...), custom_call_target="tpu_custom_call" | custom-call | tf_op jit(solution)/shard_map/pallas_call | solution.py:289
  354.1 1.0 copy-done.1
  355.0 2.3 shard_map.58
  (28 shorter events, 1.0 us)
Async XLA Ops:
  4.2 59.9 %all-to-all-start.1 = ((bf16[32,128,256]{2,1,0:T(8,128)(2,1)}), bf16[32,128,256]{2,1,0:T(8,128)(2,1)S(1)}, u32[]{:S(2)}, u32[]{:S(2)}) async-start(bf16[32,128,256]{2,1,0:T(8,128)(2,1)} %pack_kv_out.1), calls=%async_computation.1 | async-start | bytes 4194304 | tf_op jit(solution)/shard_map/all_to_all | solution.py:201
  64.1 56.8 %copy-start = (bf16[32,128,256]{2,1,0:T(8,128)(2,1)}, bf16[32,128,256]{2,1,0:T(8,128)(2,1)S(1)}, u32[]{:S(2)}) copy-start(bf16[32,128,256]{2,1,0:T(8,128)(2,1)S(1)} %all-to-all-done.1.got) | copy-start | bytes 6291460
  120.9 16.1 %copy-start.9 = (s32[512]{0:T(512)S(1)}, s32[512]{0:T(512)}, u32[]{:S(2)}) copy-start(s32[512]{0:T(512)} %param.9) | copy-start | bytes 6148
  120.9 164.2 %all-to-all-start.3 = ((bf16[32,96,1024]{2,1,0:T(8,128)(2,1)}), bf16[32,96,1024]{2,1,0:T(8,128)(2,1)}, u32[]{:S(2)}, u32[]{:S(2)}) async-start(bf16[32,96,1024]{2,1,0:T(8,128)(2,1)} %get-tuple-element.16), calls=%async_computation.3 | async-start | bytes 12582912 | tf_op jit(solution)/shard_map/all_to_all | solution.py:219
  133.7 142.8 %collective-permute-start = (bf16[7,128,256]{2,1,0:T(8,128)(2,1)S(1)}, bf16[7,128,256]{2,1,0:T(8,128)(2,1)S(1)}, u32[]{:S(2)}, u32[]{:S(2)}) collective-permute-start(bf16[7,128,256]{2,1,0:T(8,128)(2,1)S(1)} %slice.44), channel_id=1, source_target_pairs={{0,8},{8,16},{16,24},{24,32},{32,40},{40,48},{48,56},{56,64},{64,7... | collective-permute-start | bytes 1376264 | tf_op jit(solution)/shard_map/ppermute | solution.py:242
  276.5 0.8 copy-start.2
  285.1 68.9 %all-to-all-start.2 = ((bf16[8,64,1024]{2,1,0:T(8,128)(2,1)}), bf16[8,64,1024]{2,1,0:T(8,128)(2,1)S(1)}, u32[]{:S(2)}, u32[]{:S(2)}) async-start(bf16[8,64,1024]{2,1,0:T(8,128)(2,1)} %bitcast.9), calls=%async_computation.2 | async-start | bytes 2097152 | tf_op jit(solution)/shard_map/all_to_all | solution.py:280
  307.1 5.8 %collective-permute-start.1 = (bf16[2,96,1024]{2,1,0:T(8,128)(2,1)}, bf16[2,96,1024]{2,1,0:T(8,128)(2,1)S(1)}, u32[]{:S(2)}, u32[]{:S(2)}) collective-permute-start(bf16[2,96,1024]{2,1,0:T(8,128)(2,1)} %get-tuple-element.18), channel_id=1, source_target_pairs={{0,1},{1,0},{2,3},{3,2},{4,5},{5,4},{6,7},{7,6},{8,9},{9,8},{10,11... | collective-permute-start | bytes 1179656 | tf_op jit(solution)/shard_map/ppermute | solution.py:277
  308.0 12.2 %collective-permute-start.2 = (bf16[2,96,1024]{2,1,0:T(8,128)(2,1)}, bf16[2,96,1024]{2,1,0:T(8,128)(2,1)S(1)}, u32[]{:S(2)}, u32[]{:S(2)}) collective-permute-start(bf16[2,96,1024]{2,1,0:T(8,128)(2,1)} %get-tuple-element.19), channel_id=1, source_target_pairs={{0,2},{1,3},{2,0},{3,1},{4,6},{5,7},{6,4},{7,5},{8,10},{9,11},{10,... | collective-permute-start | bytes 1179656 | tf_op jit(solution)/shard_map/ppermute | solution.py:277
  309.6 18.2 %collective-permute-start.3 = (bf16[2,96,1024]{2,1,0:T(8,128)(2,1)}, bf16[2,96,1024]{2,1,0:T(8,128)(2,1)S(1)}, u32[]{:S(2)}, u32[]{:S(2)}) collective-permute-start(bf16[2,96,1024]{2,1,0:T(8,128)(2,1)} %get-tuple-element.20), channel_id=1, source_target_pairs={{0,3},{1,2},{2,1},{3,0},{4,7},{5,6},{6,5},{7,4},{8,11},{9,10},{10,... | collective-permute-start | bytes 1179656 | tf_op jit(solution)/shard_map/ppermute | solution.py:277
  309.6 29.8 %collective-permute-start.4 = (bf16[2,96,1024]{2,1,0:T(8,128)(2,1)}, bf16[2,96,1024]{2,1,0:T(8,128)(2,1)S(1)}, u32[]{:S(2)}, u32[]{:S(2)}) collective-permute-start(bf16[2,96,1024]{2,1,0:T(8,128)(2,1)} %get-tuple-element.21), channel_id=1, source_target_pairs={{0,4},{1,5},{2,6},{3,7},{4,0},{5,1},{6,2},{7,3},{8,12},{9,13},{10,... | collective-permute-start | bytes 1179656 | tf_op jit(solution)/shard_map/ppermute | solution.py:277
  312.8 33.8 %collective-permute-start.5 = (bf16[2,96,1024]{2,1,0:T(8,128)(2,1)}, bf16[2,96,1024]{2,1,0:T(8,128)(2,1)S(1)}, u32[]{:S(2)}, u32[]{:S(2)}) collective-permute-start(bf16[2,96,1024]{2,1,0:T(8,128)(2,1)} %get-tuple-element.22), channel_id=1, source_target_pairs={{0,5},{1,4},{2,7},{3,6},{4,1},{5,0},{6,3},{7,2},{8,13},{9,12},{10,... | collective-permute-start | bytes 1179656 | tf_op jit(solution)/shard_map/ppermute | solution.py:277
  313.0 37.4 %copy-start.3 = (bf16[2,96,1024]{2,1,0:T(8,128)(2,1)}, bf16[2,96,1024]{2,1,0:T(8,128)(2,1)S(1)}, u32[]{:S(2)}) copy-start(bf16[2,96,1024]{2,1,0:T(8,128)(2,1)S(1)} %collective-permute-done.1.refs_1_) | copy-start | bytes 1179652
  313.0 33.7 %collective-permute-start.6 = (bf16[2,96,1024]{2,1,0:T(8,128)(2,1)}, bf16[2,96,1024]{2,1,0:T(8,128)(2,1)S(1)}, u32[]{:S(2)}, u32[]{:S(2)}) collective-permute-start(bf16[2,96,1024]{2,1,0:T(8,128)(2,1)} %get-tuple-element.23), channel_id=1, source_target_pairs={{0,6},{1,7},{2,4},{3,5},{4,2},{5,3},{6,0},{7,1},{8,14},{9,15},{10,... | collective-permute-start | bytes 1179656 | tf_op jit(solution)/shard_map/ppermute | solution.py:277
  320.2 30.2 %copy-start.4 = (bf16[2,96,1024]{2,1,0:T(8,128)(2,1)}, bf16[2,96,1024]{2,1,0:T(8,128)(2,1)S(1)}, u32[]{:S(2)}) copy-start(bf16[2,96,1024]{2,1,0:T(8,128)(2,1)S(1)} %collective-permute-done.2.refs_2_) | copy-start | bytes 1179652
  320.2 30.2 %collective-permute-start.7 = (bf16[2,96,1024]{2,1,0:T(8,128)(2,1)}, bf16[2,96,1024]{2,1,0:T(8,128)(2,1)}, u32[]{:S(2)}, u32[]{:S(2)}) collective-permute-start(bf16[2,96,1024]{2,1,0:T(8,128)(2,1)} %get-tuple-element.24), channel_id=1, source_target_pairs={{0,7},{1,6},{2,5},{3,4},{4,3},{5,2},{6,1},{7,0},{8,15},{9,14},{10,... | collective-permute-start | bytes 1179656 | tf_op jit(solution)/shard_map/ppermute | solution.py:277
  327.8 22.6 %copy-start.5 = (bf16[2,96,1024]{2,1,0:T(8,128)(2,1)}, bf16[2,96,1024]{2,1,0:T(8,128)(2,1)S(1)}, u32[]{:S(2)}) copy-start(bf16[2,96,1024]{2,1,0:T(8,128)(2,1)S(1)} %collective-permute-done.3.refs_3_) | copy-start | bytes 1179652
  339.4 11.0 %copy-start.6 = (bf16[2,96,1024]{2,1,0:T(8,128)(2,1)}, bf16[2,96,1024]{2,1,0:T(8,128)(2,1)S(1)}, u32[]{:S(2)}) copy-start(bf16[2,96,1024]{2,1,0:T(8,128)(2,1)S(1)} %collective-permute-done.4.refs_4_) | copy-start | bytes 1179652
  346.6 3.8 %copy-start.7 = (bf16[2,96,1024]{2,1,0:T(8,128)(2,1)}, bf16[2,96,1024]{2,1,0:T(8,128)(2,1)S(1)}, u32[]{:S(2)}) copy-start(bf16[2,96,1024]{2,1,0:T(8,128)(2,1)S(1)} %collective-permute-done.5.refs_5_) | copy-start | bytes 1179652
  346.7 3.8 %copy-start.8 = (bf16[2,96,1024]{2,1,0:T(8,128)(2,1)}, bf16[2,96,1024]{2,1,0:T(8,128)(2,1)S(1)}, u32[]{:S(2)}) copy-start(bf16[2,96,1024]{2,1,0:T(8,128)(2,1)S(1)} %collective-permute-done.6.refs_6_) | copy-start | bytes 1179652
  354.1 1.0 copy-start.1

commit v3 on v2

--- a/solution.py
+++ b/solution.py
@@ -14,7 +14,7 @@
 DOCMAX = 8
 REACH = DOCMAX - 1
 ROWS = (96, 32)
-GROUP = (1, 4)
+GROUP = (2, 4)
 HALVES = 1
 COUNTS = (1, 2, 4, 6, 8)
 TILE = 384
@@ -25,14 +25,18 @@
 HBM = pl.BlockSpec(memory_space=pl.ANY)
 
 
-def pack_kv_out(dest, keys, values, out):
-    def one(b, carry):
-        s = dest[b]
-        out[s, :, :HEAD_SIZE] = keys[b]
-        out[s, :, HEAD_SIZE:] = values[b]
-        return carry
-
-    lax.fori_loop(0, keys.shape[0], one, 0)
+def pack_kv_out(dest, keys, values, out, sems):
+    copies = []
+    for b in range(keys.shape[0]):
+        for i, array in enumerate((keys, values)):
+            columns = pl.ds(i * HEAD_SIZE, HEAD_SIZE)
+            copies.append(
+                pltpu.make_async_copy(array.at[b], out.at[dest[b], :, columns], sems.at[i, b])
+            )
+    for copy in copies:
+        copy.start()
+    for copy in copies:
+        copy.wait()
 
 
 def pack_queries(dest, queries, *outs):
@@ -85,10 +89,17 @@
     step = max(d for d in range(1, heads + 1) if heads % d == 0 and d * rows <= TILE)
     row_of = row0 + lax.broadcasted_iota(jnp.int32, (step * rows, BLK), 0) % rows
     allowed = lax.broadcasted_iota(jnp.int32, (step * rows, BLK), 1) <= row_of
-    for load in loads:
-        load.wait()
+    if spread:
+        for load in loads:
+            load.wait()
 
     def some(i, carry):
+        if not spread:
+            for g in range(group):
+                at = i * group + g
+                pltpu.make_async_copy(
+                    got.at[owner[block_at(at)]], queries.at[at], q_sems.at[at]
+                ).wait()
         held = [(i * group + g, block_at(i * group + g)) for g in range(group)]
         most = count[held[0][1]]
         for _, b in held[1:]:
@@ -195,7 +206,8 @@
         pack_kv_out,
         out_shape=jax.ShapeDtypeStruct((shards, BLK, 2 * HEAD_SIZE), dtype),
         in_specs=[SMEM, VMEM, VMEM],
-        out_specs=VMEM,
+        out_specs=HBM,
+        scratch_shapes=[pltpu.SemaphoreType.DMA((2, blocks))],
         name="pack_kv_out",
     )(dest, keys.reshape(blocks, BLK, HEAD_SIZE), values.reshape(blocks, BLK, HEAD_SIZE))
     kv_got = lax.all_to_all(kv_out, "ctx", split_axis=0, concat_axis=0, tiled=True)

time: 363 us -> 362 us (level)
  no operation moved by 1% of the time
where the time goes in v3:
time: 362 us; the launch traced here: 355 us
  waiting for transfers between devices  209 us (58%)
  blocking collectives  56.8 us (16%)
  Pallas kernels  46.2 us (13%)
  starting transfers between devices  35.5 us (10%)
  other arithmetic  4.68 us (1%)
    ppermute x1, waiting for transfers between devices, exchange(): halo = lax.ppermute(packed[blocks - REACH:], 'ctx', route)  138 us
    all_to_all x1, blocking collectives, exchange(): lax.all_to_all(q, 'ctx', split_axis=0, concat_axis=0, tiled=True)  56.8 us
    all_to_all x1, waiting for transfers between devices, exchange(): lax.all_to_all(kv_out, 'ctx', split_axis=0, concat_axis=0, tiled=True)  38 us
    ppermute x7, waiting for transfers between devices, exchange(): parts[k] = lax.ppermute(part, 'head', swap) if k else part  33.2 us
    pallas_call x2, Pallas kernels, exchange(): pl.pallas_call(functools.partial(attend, row0, GROUP[r], first if spread...  23.9 us
    all_to_all x1, starting transfers between devices, exchange(): lax.all_to_all(kv_out, 'ctx', split_axis=0, concat_axis=0, tiled=True)  11.1 us
    pallas_call x1, Pallas kernels, exchange(): pl.pallas_call(pack_queries, out_shape=[jax.ShapeDtypeStruct((shards, row...  10.8 us
    ppermute x7, starting transfers between devices, exchange(): parts[k] = lax.ppermute(part, 'head', swap) if k else part  9.89 us
  transfers between devices with their start and end apart: 11, of which 7 were waited for; matrix products, arithmetic and copies ran while one was open for 1% of the time, Pallas kernels for 12%

profile of v3, /device:TPU:48, one launch (start us, length us, event | category | flops | bytes accessed | tf_op | source)
XLA Modules:
  0.0 355.5 jit_solution(6392967635622791469)
XLA Ops:
  0.0 0.9 select_reduce_fusion
  1.4 2.5 pack_kv_out.1
  3.9 11.1 %all-to-all-start.1 = ((bf16[32,128,256]{2,1,0:T(8,128)(2,1)}), bf16[32,128,256]{2,1,0:T(8,128)(2,1)S(1)}, u32[]{:S(2)}, u32[]{:S(2)}) async-start(bf16[32,128,256]{2,1,0:T(8,128)(2,1)} %pack_kv_out.1), calls=%async_computation.1 | async-start | bytes 4194304 | tf_op jit(solution)/shard_map/all_to_all | solution.py:213
  15.0 10.8 %pack_queries.1 = (bf16[32,96,1024]{2,1,0:T(8,128)(2,1)}, bf16[32,32,1024]{2,1,0:T(8,128)(2,1)}) custom-call(s32[16]{0:T(128)} %and_select_fusion.dest, bf16[16,128,1024]{2,1,0:T(8,128)(2,1)} %bitcast.8), custom_call_target="tpu_custom_call" | custom-call | tf_op jit(solution)/shard_map/pack_queries/pallas_call | solution.py:216
  25.8 38.0 %all-to-all-done.1.got = bf16[32,128,256]{2,1,0:T(8,128)(2,1)S(1)} async-done(((bf16[32,128,256]{2,1,0:T(8,128)(2,1)}), bf16[32,128,256]{2,1,0:T(8,128)(2,1)S(1)}, u32[]{:S(2)}, u32[]{:S(2)}) %all-to-all-start.1) | async-done | bytes 2097184 | tf_op jit(solution)/shard_map/all_to_all | solution.py:213
  63.8 56.8 %all_to_all.20.got = bf16[32,32,1024]{2,1,0:T(8,128)(2,1)} all-to-all(bf16[32,32,1024]{2,1,0:T(8,128)(2,1)} %get-tuple-element.15), channel_id=1, replica_groups=mesh['ctx'=32,'head'=8] {'ctx'}, dimensions={0} | all-to-all | bytes 4194304 | tf_op jit(solution)/shard_map/all_to_all | solution.py:231
  120.6 6.8 %all-to-all-start.3 = ((bf16[32,96,1024]{2,1,0:T(8,128)(2,1)}), bf16[32,96,1024]{2,1,0:T(8,128)(2,1)}, u32[]{:S(2)}, u32[]{:S(2)}) async-start(bf16[32,96,1024]{2,1,0:T(8,128)(2,1)} %get-tuple-element.16), calls=%async_computation.3 | async-start | bytes 12582912 | tf_op jit(solution)/shard_map/all_to_all | solution.py:231
  127.4 1.3 and_select_fusion.1.owner
  128.7 0.6 pad_add_fusion.spot
  129.3 3.0 pack_kv_in.1.packed
  132.3 1.1 slice.44
  133.3 3.4 collective-permute-start
  136.8 0.7 iota_add_fusion.1
  137.7 0.6 select_reduce_fusion.1.turn
  138.3 137.9 %collective-permute-done.halo = bf16[7,128,256]{2,1,0:T(8,128)(2,1)S(1)} collective-permute-done((bf16[7,128,256]{2,1,0:T(8,128)(2,1)S(1)}, bf16[7,128,256]{2,1,0:T(8,128)(2,1)S(1)}, u32[]{:S(2)}, u32[]{:S(2)}) %collective-permute-start) | collective-permute-done | bytes 458784 | tf_op jit(solution)/shard_map/ppermute | solution.py:254
  276.2 0.8 copy-done.2
  277.0 7.5 %shard_map.55 = bf16[16,32,1024]{2,1,0:T(8,128)(2,1)} custom-call(s32[2]{0:T(128)} %pad_add_fusion.spot, s32[16]{0:T(128)} %and_select_fusion.1.owner, s32[16]{0:T(128)} %get-tuple-element.26.count, s32[16]{0:T(128)} %select_reduce_fusion.1.turn, bf16[32,32,1024]{2,1,0:T(8,128)(2,1)} %all_to_all.20.got, bf16[16,128,256]{2,1,0:T(8,128)(2,1)} %pack_kv_in.1.packed, ...), custom_call_target="tpu_custom_call" | custom-call | tf_op jit(solution)/shard_map/pallas_call | solution.py:278
  284.5 4.3 %all-to-all-start.2 = ((bf16[8,64,1024]{2,1,0:T(8,128)(2,1)}), bf16[8,64,1024]{2,1,0:T(8,128)(2,1)S(1)}, u32[]{:S(2)}, u32[]{:S(2)}) async-start(bf16[8,64,1024]{2,1,0:T(8,128)(2,1)} %bitcast.9), calls=%async_computation.2 | async-start | bytes 2097152 | tf_op jit(solution)/shard_map/all_to_all | solution.py:292
  288.8 16.4 %shard_map.56 = (bf16[2,96,1024]{2,1,0:T(8,128)(2,1)}, bf16[2,96,1024]{2,1,0:T(8,128)(2,1)}, bf16[2,96,1024]{2,1,0:T(8,128)(2,1)}, bf16[2,96,1024]{2,1,0:T(8,128...) custom-call(s32[2]{0:T(128)} %pad_add_fusion.spot, ...), custom_call_target="tpu_custom_call" | custom-call | tf_op jit(solution)/shard_map/pallas_call | solution.py:278
  305.3 0.6 collective-permute-start.1
  305.9 1.6 collective-permute-start.2
  307.5 3.2 collective-permute-start.4
  310.9 2.8 collective-permute-start.6
  313.7 4.3 %collective-permute-done.2.refs_2_ = bf16[2,96,1024]{2,1,0:T(8,128)(2,1)S(1)} collective-permute-done((bf16[2,96,1024]{2,1,0:T(8,128)(2,1)}, bf16[2,96,1024]{2,1,0:T(8,128)(2,1)S(1)}, u32[]{:S(2)}, u32[]{:S(2)}) %collective-permute-start.2) | collective-permute-done | bytes 393248 | tf_op jit(solution)/shard_map/ppermute | solution.py:289
  318.1 1.4 collective-permute-start.7
  319.5 6.2 %collective-permute-done.3.refs_3_ = bf16[2,96,1024]{2,1,0:T(8,128)(2,1)S(1)} collective-permute-done((bf16[2,96,1024]{2,1,0:T(8,128)(2,1)}, bf16[2,96,1024]{2,1,0:T(8,128)(2,1)S(1)}, u32[]{:S(2)}, u32[]{:S(2)}) %collective-permute-start.3) | collective-permute-done | bytes 393248 | tf_op jit(solution)/shard_map/ppermute | solution.py:289
  325.7 11.5 %collective-permute-done.4.refs_4_ = bf16[2,96,1024]{2,1,0:T(8,128)(2,1)S(1)} collective-permute-done((bf16[2,96,1024]{2,1,0:T(8,128)(2,1)}, bf16[2,96,1024]{2,1,0:T(8,128)(2,1)S(1)}, u32[]{:S(2)}, u32[]{:S(2)}) %collective-permute-start.4) | collective-permute-done | bytes 393248 | tf_op jit(solution)/shard_map/ppermute | solution.py:289
  337.3 7.3 %collective-permute-done.5.refs_5_ = bf16[2,96,1024]{2,1,0:T(8,128)(2,1)S(1)} collective-permute-done((bf16[2,96,1024]{2,1,0:T(8,128)(2,1)}, bf16[2,96,1024]{2,1,0:T(8,128)(2,1)S(1)}, u32[]{:S(2)}, u32[]{:S(2)}) %collective-permute-start.5) | collective-permute-done | bytes 393248 | tf_op jit(solution)/shard_map/ppermute | solution.py:289
  344.6 3.7 %collective-permute-done.7.refs_7_ = bf16[2,96,1024]{2,1,0:T(8,128)(2,1)} collective-permute-done((bf16[2,96,1024]{2,1,0:T(8,128)(2,1)}, bf16[2,96,1024]{2,1,0:T(8,128)(2,1)}, u32[]{:S(2)}, u32[]{:S(2)}) %collective-permute-start.7) | collective-permute-done | bytes 393248 | tf_op jit(solution)/shard_map/ppermute | solution.py:289
  348.4 3.6 %shard_map.57.refs_1_ = bf16[256,8192]{1,0:T(8,128)(2,1)} custom-call(s32[2]{0:T(128)} %pad_add_fusion.spot, bf16[2,96,1024]{2,1,0:T(8,128)(2,1)} %get-tuple-element.17.refs_0_, bf16[2,96,1024]{2,1,0:T(8,128)(2,1)} %copy-done.3, bf16[2,96,1024]{2,1,0:T(8,128)(2,1)} %copy-done.4, bf16[2,96,1024]{2,1,0:T(8,128)(2,1)} %copy-done.5, ...), custom_call_target="tpu_custom_call" | custom-call | tf_op jit(solution)/shard_map/pallas_call | solution.py:301
  352.0 1.0 copy-done.1
  353.0 2.3 shard_map.58
  (28 shorter events, 0.9 us)
Async XLA Ops:
  3.9 59.9 %all-to-all-start.1 = ((bf16[32,128,256]{2,1,0:T(8,128)(2,1)}), bf16[32,128,256]{2,1,0:T(8,128)(2,1)S(1)}, u32[]{:S(2)}, u32[]{:S(2)}) async-start(bf16[32,128,256]{2,1,0:T(8,128)(2,1)} %pack_kv_out.1), calls=%async_computation.1 | async-start | bytes 4194304 | tf_op jit(solution)/shard_map/all_to_all | solution.py:213
  63.8 56.8 %copy-start = (bf16[32,128,256]{2,1,0:T(8,128)(2,1)}, bf16[32,128,256]{2,1,0:T(8,128)(2,1)S(1)}, u32[]{:S(2)}) copy-start(bf16[32,128,256]{2,1,0:T(8,128)(2,1)S(1)} %all-to-all-done.1.got) | copy-start | bytes 6291460
  120.6 16.1 %copy-start.9 = (s32[512]{0:T(512)S(1)}, s32[512]{0:T(512)}, u32[]{:S(2)}) copy-start(s32[512]{0:T(512)} %param.9) | copy-start | bytes 6148
  120.6 163.9 %all-to-all-start.3 = ((bf16[32,96,1024]{2,1,0:T(8,128)(2,1)}), bf16[32,96,1024]{2,1,0:T(8,128)(2,1)}, u32[]{:S(2)}, u32[]{:S(2)}) async-start(bf16[32,96,1024]{2,1,0:T(8,128)(2,1)} %get-tuple-element.16), calls=%async_computation.3 | async-start | bytes 12582912 | tf_op jit(solution)/shard_map/all_to_all | solution.py:231
  133.3 142.8 %collective-permute-start = (bf16[7,128,256]{2,1,0:T(8,128)(2,1)S(1)}, bf16[7,128,256]{2,1,0:T(8,128)(2,1)S(1)}, u32[]{:S(2)}, u32[]{:S(2)}) collective-permute-start(bf16[7,128,256]{2,1,0:T(8,128)(2,1)S(1)} %slice.44), channel_id=1, source_target_pairs={{0,8},{8,16},{16,24},{24,32},{32,40},{40,48},{48,56},{56,64},{64,7... | collective-permute-start | bytes 1376264 | tf_op jit(solution)/shard_map/ppermute | solution.py:254
  276.2 0.8 copy-start.2
  284.5 67.5 %all-to-all-start.2 = ((bf16[8,64,1024]{2,1,0:T(8,128)(2,1)}), bf16[8,64,1024]{2,1,0:T(8,128)(2,1)S(1)}, u32[]{:S(2)}, u32[]{:S(2)}) async-start(bf16[8,64,1024]{2,1,0:T(8,128)(2,1)} %bitcast.9), calls=%async_computation.2 | async-start | bytes 2097152 | tf_op jit(solution)/shard_map/all_to_all | solution.py:292
  305.3 5.6 %collective-permute-start.1 = (bf16[2,96,1024]{2,1,0:T(8,128)(2,1)}, bf16[2,96,1024]{2,1,0:T(8,128)(2,1)S(1)}, u32[]{:S(2)}, u32[]{:S(2)}) collective-permute-start(bf16[2,96,1024]{2,1,0:T(8,128)(2,1)} %get-tuple-element.18), channel_id=1, source_target_pairs={{0,1},{1,0},{2,3},{3,2},{4,5},{5,4},{6,7},{7,6},{8,9},{9,8},{10,11... | collective-permute-start | bytes 1179656 | tf_op jit(solution)/shard_map/ppermute | solution.py:289
  305.9 12.2 %collective-permute-start.2 = (bf16[2,96,1024]{2,1,0:T(8,128)(2,1)}, bf16[2,96,1024]{2,1,0:T(8,128)(2,1)S(1)}, u32[]{:S(2)}, u32[]{:S(2)}) collective-permute-start(bf16[2,96,1024]{2,1,0:T(8,128)(2,1)} %get-tuple-element.19), channel_id=1, source_target_pairs={{0,2},{1,3},{2,0},{3,1},{4,6},{5,7},{6,4},{7,5},{8,10},{9,11},{10,... | collective-permute-start | bytes 1179656 | tf_op jit(solution)/shard_map/ppermute | solution.py:289
  307.5 18.2 %collective-permute-start.3 = (bf16[2,96,1024]{2,1,0:T(8,128)(2,1)}, bf16[2,96,1024]{2,1,0:T(8,128)(2,1)S(1)}, u32[]{:S(2)}, u32[]{:S(2)}) collective-permute-start(bf16[2,96,1024]{2,1,0:T(8,128)(2,1)} %get-tuple-element.20), channel_id=1, source_target_pairs={{0,3},{1,2},{2,1},{3,0},{4,7},{5,6},{6,5},{7,4},{8,11},{9,10},{10,... | collective-permute-start | bytes 1179656 | tf_op jit(solution)/shard_map/ppermute | solution.py:289
  307.5 29.8 %collective-permute-start.4 = (bf16[2,96,1024]{2,1,0:T(8,128)(2,1)}, bf16[2,96,1024]{2,1,0:T(8,128)(2,1)S(1)}, u32[]{:S(2)}, u32[]{:S(2)}) collective-permute-start(bf16[2,96,1024]{2,1,0:T(8,128)(2,1)} %get-tuple-element.21), channel_id=1, source_target_pairs={{0,4},{1,5},{2,6},{3,7},{4,0},{5,1},{6,2},{7,3},{8,12},{9,13},{10,... | collective-permute-start | bytes 1179656 | tf_op jit(solution)/shard_map/ppermute | solution.py:289
  310.7 33.9 %collective-permute-start.5 = (bf16[2,96,1024]{2,1,0:T(8,128)(2,1)}, bf16[2,96,1024]{2,1,0:T(8,128)(2,1)S(1)}, u32[]{:S(2)}, u32[]{:S(2)}) collective-permute-start(bf16[2,96,1024]{2,1,0:T(8,128)(2,1)} %get-tuple-element.22), channel_id=1, source_target_pairs={{0,5},{1,4},{2,7},{3,6},{4,1},{5,0},{6,3},{7,2},{8,13},{9,12},{10,... | collective-permute-start | bytes 1179656 | tf_op jit(solution)/shard_map/ppermute | solution.py:289
  310.9 37.5 %copy-start.3 = (bf16[2,96,1024]{2,1,0:T(8,128)(2,1)}, bf16[2,96,1024]{2,1,0:T(8,128)(2,1)S(1)}, u32[]{:S(2)}) copy-start(bf16[2,96,1024]{2,1,0:T(8,128)(2,1)S(1)} %collective-permute-done.1.refs_1_) | copy-start | bytes 1179652
  310.9 33.7 %collective-permute-start.6 = (bf16[2,96,1024]{2,1,0:T(8,128)(2,1)}, bf16[2,96,1024]{2,1,0:T(8,128)(2,1)S(1)}, u32[]{:S(2)}, u32[]{:S(2)}) collective-permute-start(bf16[2,96,1024]{2,1,0:T(8,128)(2,1)} %get-tuple-element.23), channel_id=1, source_target_pairs={{0,6},{1,7},{2,4},{3,5},{4,2},{5,3},{6,0},{7,1},{8,14},{9,15},{10,... | collective-permute-start | bytes 1179656 | tf_op jit(solution)/shard_map/ppermute | solution.py:289
  318.1 30.3 %copy-start.4 = (bf16[2,96,1024]{2,1,0:T(8,128)(2,1)}, bf16[2,96,1024]{2,1,0:T(8,128)(2,1)S(1)}, u32[]{:S(2)}) copy-start(bf16[2,96,1024]{2,1,0:T(8,128)(2,1)S(1)} %collective-permute-done.2.refs_2_) | copy-start | bytes 1179652
  318.1 30.3 %collective-permute-start.7 = (bf16[2,96,1024]{2,1,0:T(8,128)(2,1)}, bf16[2,96,1024]{2,1,0:T(8,128)(2,1)}, u32[]{:S(2)}, u32[]{:S(2)}) collective-permute-start(bf16[2,96,1024]{2,1,0:T(8,128)(2,1)} %get-tuple-element.24), channel_id=1, source_target_pairs={{0,7},{1,6},{2,5},{3,4},{4,3},{5,2},{6,1},{7,0},{8,15},{9,14},{10,... | collective-permute-start | bytes 1179656 | tf_op jit(solution)/shard_map/ppermute | solution.py:289
  325.7 22.6 %copy-start.5 = (bf16[2,96,1024]{2,1,0:T(8,128)(2,1)}, bf16[2,96,1024]{2,1,0:T(8,128)(2,1)S(1)}, u32[]{:S(2)}) copy-start(bf16[2,96,1024]{2,1,0:T(8,128)(2,1)S(1)} %collective-permute-done.3.refs_3_) | copy-start | bytes 1179652
  337.3 11.0 %copy-start.6 = (bf16[2,96,1024]{2,1,0:T(8,128)(2,1)}, bf16[2,96,1024]{2,1,0:T(8,128)(2,1)S(1)}, u32[]{:S(2)}) copy-start(bf16[2,96,1024]{2,1,0:T(8,128)(2,1)S(1)} %collective-permute-done.4.refs_4_) | copy-start | bytes 1179652
  344.6 3.7 %copy-start.7 = (bf16[2,96,1024]{2,1,0:T(8,128)(2,1)}, bf16[2,96,1024]{2,1,0:T(8,128)(2,1)S(1)}, u32[]{:S(2)}) copy-start(bf16[2,96,1024]{2,1,0:T(8,128)(2,1)S(1)} %collective-permute-done.5.refs_5_) | copy-start | bytes 1179652
  344.6 3.7 %copy-start.8 = (bf16[2,96,1024]{2,1,0:T(8,128)(2,1)}, bf16[2,96,1024]{2,1,0:T(8,128)(2,1)S(1)}, u32[]{:S(2)}) copy-start(bf16[2,96,1024]{2,1,0:T(8,128)(2,1)S(1)} %collective-permute-done.6.refs_6_) | copy-start | bytes 1179652
  352.0 1.0 copy-start.1
